TPU v7x, 32 devices: a whole 2x2x4 slice. The times are simulated.
32 devices in a mesh: shard: 4 (over y, x), replica: 8 (over z, core).
Axes of the slice: x: 2, y: 2, z: 4, core: 2. Of those that a mesh axis runs over, the one named last changes fastest.
Arguments:
- tokens: bfloat16 [8192, 1536], P(('shard', 'replica')), may hold values from -6 to 6
- cotangent: bfloat16 [8192, 1536], P(('shard', 'replica')), may hold values from -6 to 6
- seq_lengths: int32 [64], replicated, may hold values from 0 to 256, as said below
- seq_device: int32 [64], replicated, may hold values from 0 to 31
- seq_offsets: int32 [64], replicated, may hold values from 0 to 1
- norm_attn: bfloat16 [1, 1536], P(None, 'shard'), may hold values from 0.5 to 1.5
- w_qkv: bfloat16 [1, 1536, 3072], P(None, 'shard'), may hold values from -0.15625 to 0.15625
- w_out: bfloat16 [1, 1536, 1536], P(None, 'shard'), may hold values from -0.625 to 0.625
- norm_mlp: bfloat16 [1, 1536], P(None, 'shard'), may hold values from 0.5 to 1.5
- w_gate_up: bfloat16 [1, 1536, 8192], P(None, 'shard'), may hold values from -0.15625 to 0.15625
- w_down: bfloat16 [1, 4096, 1536], P(None, 'shard'), may hold values from -0.125 to 0.125
Outputs:
- result: bfloat16 [8192, 1536], P(('shard', 'replica'))
- grad_tokens: float32 [8192, 1536], P(('shard', 'replica'))
- grad_norm_attn: float32 [1, 1536], P(None, 'shard')
- grad_w_qkv: float32 [1, 1536, 3072], P(None, 'shard')
- grad_w_out: float32 [1, 1536, 1536], P(None, 'shard')
- grad_norm_mlp: float32 [1, 1536], P(None, 'shard')
- grad_w_gate_up: float32 [1, 1536, 8192], P(None, 'shard')
- grad_w_down: float32 [1, 4096, 1536], P(None, 'shard')
Inputs may be any that keep to these rules, and one draw needn't show every extreme that they name: `seq_lengths`: each device is named by exactly 2 entries. A sequence lies within blocks 2p and 2p + 1 of its device for some p; sequences of one device never share a row; length 0 marks an unused entry. In every draw some device is full, its every pair of blocks holding one sequence of length 256.
All inputs are finite; a program needn't handle non-finite values.
Results may differ from a plain program's by a relative error of at most 0.02.
Values may be sent and summed in bfloat16 or wider, within the bound.
A program may use at most 320 MiB of HBM per device.

v0:
```python
import functools

import jax
import jax.numpy as jnp
from jax import lax
from jax.experimental import pallas as pl
from jax.experimental.pallas import tpu as pltpu
from jax.sharding import PartitionSpec as P

HEADS = 16
KV_HEADS = 8
HEAD = 96
FF = 4096
BLOCK = 128

epsilon = 1e-05
rope_base = 100000.0


def rms_scale(field):
    return lax.rsqrt(jnp.mean(field * field, axis=-1, keepdims=True) + epsilon)


def rotate(field):
    half = field.shape[-1] // 2
    return jnp.concatenate([-field[..., half:], field[..., :half]], axis=-1)


def rope_tables(position):
    half = HEAD // 2
    freqs = rope_base ** (-(jnp.arange(half, dtype=jnp.float32) * 2.0) / HEAD)
    angles = position.astype(jnp.float32)[:, None] * freqs[None, :]
    cosine = jnp.cos(angles)
    sine = jnp.sin(angles)
    return (jnp.concatenate([cosine, cosine], axis=-1), jnp.concatenate([sine, sine], axis=-1))


def locate(device, seq_lengths, seq_device, seq_offsets, rows):
    starts = seq_offsets * BLOCK
    local = jnp.arange(rows, dtype=jnp.int32)
    labels = jnp.arange(seq_lengths.shape[0], dtype=jnp.int32)
    hits = (
        (seq_device[None, :] == device)
        & (local[:, None] >= starts[None, :])
        & (local[:, None] < (starts + seq_lengths)[None, :])
    )
    segment = jnp.max(jnp.where(hits, labels[None, :], -1), axis=1)
    begin = jnp.sum(jnp.where(hits, starts[None, :], 0), axis=1)
    return (segment, local - begin)


def mask_of(segment):
    local = jnp.arange(segment.shape[0], dtype=jnp.int32)
    return (segment[:, None] == segment[None, :]) & (local[None, :] <= local[:, None])


def contract_rows(left, right):
    return lax.dot_general(
        left, right, (((0,), (0,)), ((), ())), preferred_element_type=jnp.float32
    )


def contract_cols(left, right):
    return lax.dot_general(
        left, right, (((1,), (1,)), ((), ())), preferred_element_type=jnp.float32
    )


def norm_back(grad_normed, field, scale, gain):
    normed = field * scale
    grad_gain = jnp.sum(grad_normed * normed, axis=0)
    inner = grad_normed * gain[None, :]
    grad_field = scale * (inner - normed * jnp.mean(inner * normed, axis=-1, keepdims=True))
    return (grad_field, grad_gain)


def join_grads(grad_queries, grad_keys, grad_values, cosine, sine):
    rows = grad_queries.shape[0]
    grad_queries = grad_queries * cosine[:, None, :] - rotate(grad_queries * sine[:, None, :])
    grad_keys = grad_keys * cosine[:, None, :] - rotate(grad_keys * sine[:, None, :])
    return jnp.concatenate(
        [
            grad_queries.reshape(rows, -1),
            grad_keys.reshape(rows, -1),
            grad_values.reshape(rows, -1),
        ],
        axis=1,
    ).astype(jnp.bfloat16)


def attention_scores(queries_b, keys_b, allowed):
    rows = queries_b.shape[0]
    kv_count = keys_b.shape[1]
    grouped = queries_b.reshape(rows, kv_count, queries_b.shape[1] // kv_count, HEAD)
    scores = jnp.einsum(
        "qkgd,pkd->kgqp", grouped, keys_b, preferred_element_type=jnp.float32
    ) * HEAD ** (-0.5)
    return jnp.where(allowed, scores, -1e30)


def attend_backward(grad_mixed_b, queries_b, keys_b, values_b, total, allowed):
    rows = queries_b.shape[0]
    q_heads = queries_b.shape[1]
    kv_count = keys_b.shape[1]
    per = q_heads // kv_count
    factor = HEAD ** (-0.5)
    grad_mixed = grad_mixed_b.reshape(rows, kv_count, per, HEAD)
    weights = jnp.exp(attention_scores(queries_b, keys_b, allowed) - total)
    weights_b = weights.astype(jnp.bfloat16)
    grad_values = jnp.einsum(
        "kgqp,qkgd->pkd", weights_b, grad_mixed, preferred_element_type=jnp.float32
    )
    grad_weights = jnp.einsum(
        "qkgd,pkd->kgqp", grad_mixed, values_b, preferred_element_type=jnp.float32
    )
    grad_scores = weights * (grad_weights - jnp.sum(weights * grad_weights, axis=-1, keepdims=True))
    grad_scores_b = grad_scores.astype(jnp.bfloat16)
    grouped = queries_b.reshape(rows, kv_count, per, HEAD)
    grad_queries = jnp.einsum(
        "kgqp,pkd->qkgd", grad_scores_b, keys_b, preferred_element_type=jnp.float32
    )
    grad_queries = grad_queries.reshape(rows, q_heads, HEAD) * factor
    grad_keys = (
        jnp.einsum("kgqp,qkgd->pkd", grad_scores_b, grouped, preferred_element_type=jnp.float32)
        * factor
    )
    return (grad_queries, grad_keys, grad_values)


def gate_back(grad_hidden, gate, upper):
    sigma = jax.nn.sigmoid(gate)
    grad_gate = grad_hidden * upper * sigma * (1.0 + gate * (1.0 - sigma))
    grad_upper = grad_hidden * (gate * sigma)
    return (grad_gate.astype(jnp.bfloat16), grad_upper.astype(jnp.bfloat16))


MESH = pl.DeviceIdType.MESH


def submasks(order, step):
    masks = [0]
    for bit in order[:step]:
        masks += [mask | bit for mask in masks]
    return masks


def greet(partners):
    barrier = pltpu.get_barrier_semaphore()
    for partner in partners:
        pl.semaphore_signal(barrier, inc=1, device_id=partner, device_id_type=MESH)
    pl.semaphore_wait(barrier, len(partners))


class Item:
    def __init__(self, n_shard, own, full, cols, single, sems):
        self.shard, replica = lax.axis_index("shard"), lax.axis_index("replica")
        self.replica = replica
        core, pair = lax.rem(replica, 2), lax.rem(replica // 2, 2)
        self.bits = [1 << i for i in range(n_shard.bit_length() - 1)]
        self.n_shard = n_shard
        self.own, self.full, self.cols = own, full, cols
        self.rows = own.shape[0]
        self.load_sem, self.local_sem, self.send_sem, self.recv_sem = sems
        half = self.rows // 2
        common = half - 2 * single
        base = core * half
        self.parts = [
            (base + pair * (single + common), single, self.bits),
            (base + single, common, self.bits[1:] + self.bits[:1]),
        ]
        self.mate = (base + (1 - pair) * (single + common), single)
        self.half = (base, half)
        self.other_half = ((1 - core) * half, half)
        self.number = {}
        self.waited, self.started = set(), {}

    def index(self, key):
        return self.number.setdefault(key, len(self.number))

    def window(self, mask, span):
        start = pl.multiple_of((self.shard ^ mask) * self.rows + span[0], 16)
        return self.full.at[pl.ds(start, span[1]), self.cols]

    def send(self, key, src, dst, device):
        if key in self.started:
            return
        index = self.index(key)
        copy = pltpu.make_async_remote_copy(
            src_ref=src,
            dst_ref=dst,
            send_sem=self.send_sem.at[index],
            recv_sem=self.recv_sem.at[index],
            device_id=device,
            device_id_type=MESH,
        )
        copy.start()
        self.started[key] = copy

    def landed(self, key, span):
        if key in self.waited:
            return
        self.waited.add(key)
        window = self.window(key[2], span)
        pltpu.make_async_remote_copy(
            src_ref=window,
            dst_ref=window,
            send_sem=self.send_sem.at[self.index(key)],
            recv_sem=self.recv_sem.at[self.index(key)],
            device_id={"replica": self.replica ^ 1},
            device_id_type=MESH,
        ).wait_recv()

    def load(self, source):
        self.loading = pltpu.make_async_copy(source.at[:, self.cols], self.own.at[:, self.cols], self.load_sem)
        self.loading.start()

    def over_shard(self, part, step, mask):
        start, size, order = self.parts[part]
        bit = order[step]
        window = self.window(mask, (start, size))
        src = window
        if mask == 0:
            src = self.own.at[pl.ds(pl.multiple_of(start, 16), size), self.cols]
        self.send(("shard", part, mask | bit), src, window, {"shard": self.shard ^ bit})

    def first(self):
        self.loading.wait()
        for step in range(len(self.bits)):
            for part in range(2):
                self.over_shard(part, step, 0)
        start = pl.multiple_of(self.shard * self.rows, 16)
        self.placing = pltpu.make_async_copy(
            self.own.at[:, self.cols], self.full.at[pl.ds(start, self.rows), self.cols], self.local_sem
        )
        self.placing.start()

    def arrive(self, part, mask):
        span = self.parts[part][:2]
        self.landed(("shard", part, mask), span)
        if part == 0:
            window = self.window(mask, span)
            self.send(("pair", 0, mask), window, window, {"replica": self.replica ^ 2})

    def relay(self):
        for step in range(1, len(self.bits)):
            for part in range(2):
                for mask in submasks(self.parts[part][2], step)[1:]:
                    self.arrive(part, mask)
                    self.over_shard(part, step, mask)

    def pass_on(self):
        for mask in range(1, self.n_shard):
            self.arrive(0, mask)

    def across(self):
        for mask in range(1, self.n_shard):
            self.arrive(1, mask)
            self.landed(("pair", 0, mask), self.mate)
            window = self.window(mask, self.half)
            self.send(("core", 0, mask), window, window, {"replica": self.replica ^ 1})

    def complete(self):
        for mask in range(1, self.n_shard):
            self.landed(("core", 0, mask), self.other_half)
        self.placing.wait()

    def finish(self):
        for copy in self.started.values():
            copy.wait_send()


def round_to(value, unit):
    return max(unit, int(value / unit + 0.5) * unit)


def scaled_rows(field):
    return field * lax.rsqrt(jnp.mean(field * field, axis=-1, keepdims=True) + epsilon)


QUAD = 4 * HEAD
TILE = 512


def forward_kernel(n_shard, plan, stages, *refs):
    refs = list(refs)
    take = lambda n: [refs.pop(0) for _ in range(n)]
    weights, (gain, tokens, cosine, sine, mask) = take(4), take(5)
    fulls = take(4)
    turned_a, turned_o, turned_m, turned_h, roped, lse, middle, gate_up, gains = take(9)
    owns, (gain_all, w_qkv, w_out, tiles) = take(4), take(4)
    field, normed, project, q_heads, k_heads, v_heads, mixed = take(7)
    out_a, out_o, out_m, out_h, out_roped, out_lse, pre = take(7)
    load_sem, local_sem, send_sem, recv_sem, gain_send, gain_recv, gain_sem, tile_sem, out_sem = take(9)
    shard, replica = lax.axis_index("shard"), lax.axis_index("replica")
    rows, model = tokens.shape
    owned = gain.shape[1]

    items = []
    for n, (weight, start, size, single) in enumerate(plan):
        item = Item(
            n_shard,
            owns[weight],
            fulls[weight],
            pl.ds(start, size),
            single,
            (load_sem.at[n], local_sem.at[n], send_sem.at[n], recv_sem.at[n]),
        )
        item.load(weights[weight])
        items.append(item)
    gain_own = pltpu.make_async_copy(gain, gain_all.at[shard], gain_sem.at[0])
    gain_own.start()
    greet(
        [{"shard": shard ^ other} for other in range(1, n_shard)]
        + [{"replica": replica ^ 1}, {"replica": replica ^ 2}]
    )

    def gain_copy(other, index):
        return pltpu.make_async_remote_copy(
            src_ref=gain,
            dst_ref=gain_all.at[index],
            send_sem=gain_send.at[other - 1],
            recv_sem=gain_recv.at[other - 1],
            device_id={"shard": shard ^ other},
            device_id_type=MESH,
        )

    for other in range(1, n_shard):
        gain_copy(other, shard).start()

    leaving = []

    def leave(src, dst):
        copy = pltpu.make_async_copy(src, dst, out_sem.at[len(leaving)])
        copy.start()
        leaving.append(copy)

    def norm(row):
        value = scaled_rows(field[...])
        for other in range(n_shard):
            span = slice(other * owned, (other + 1) * owned)
            normed[:, span] = (value[:, span] * gain_all[other, row : row + 1, :]).astype(jnp.bfloat16)

    def fetch(weight, index, start, dst):
        copy = pltpu.make_async_copy(
            fulls[weight].at[:, pl.ds(start, dst.shape[1])], dst, tile_sem.at[index]
        )
        copy.start()
        return copy

    def begin():
        gain_own.wait()
        for other in range(1, n_shard):
            gain_copy(other, shard ^ other).wait()
        leave(gain_all, gains)
        field[...] = tokens[...].astype(jnp.float32)
        norm(0)
        out_a[...] = normed[...].astype(jnp.float32).T.astype(jnp.bfloat16)
        leave(out_a, turned_a)

    def projections():
        loads = [
            fetch(0, n, n * TILE, w_qkv.at[:, pl.ds(n * TILE, TILE)])
            for n in range(w_qkv.shape[1] // TILE)
        ]
        for n, load in enumerate(loads):
            load.wait()
            span = pl.ds(n * TILE, TILE)
            project[:, span] = jnp.dot(
                normed[...], w_qkv[:, span], preferred_element_type=jnp.float32
            )

    lane = lax.broadcasted_iota(jnp.int32, (rows, QUAD), 1)
    first_half = lax.rem(lane, HEAD) < HEAD // 2
    in_head = lax.broadcasted_iota(jnp.int32, (rows, 128), 1) < HEAD

    def rope():
        for quad, heads in enumerate([q_heads] * 4 + [k_heads] * 2 + [v_heads] * 2):
            span = slice(quad * QUAD, (quad + 1) * QUAD)
            value = project[:, span]
            if quad < 6:
                turned = jnp.where(
                    first_half,
                    -pltpu.roll(value, QUAD - HEAD // 2, 1),
                    pltpu.roll(value, HEAD // 2, 1),
                )
                value = value * cosine[...] + turned * sine[...]
            out_roped[:, span] = value.astype(jnp.bfloat16)
            base = [0, 4, 8, 12, 0, 4, 0, 4][quad]
            for n in range(4):
                moved = value if n == 0 else pltpu.roll(value, QUAD - n * HEAD, 1)
                heads[base + n] = jnp.where(in_head, moved[:, :128], 0.0).astype(jnp.bfloat16)
        leave(out_roped, roped)
        out_lse[...] = jnp.zeros_like(out_lse)

    def attend(quad):
        allowed = mask[...] > 0.5
        spot = lax.broadcasted_iota(jnp.int32, (rows, 128), 1)
        total = jnp.zeros((rows, QUAD), jnp.float32)
        for n in range(4):
            query = q_heads[4 * quad + n]
            key = k_heads[2 * quad + n // 2]
            scores = lax.dot_general(
                query, key, (((1,), (1,)), ((), ())), preferred_element_type=jnp.float32
            ) * HEAD ** (-0.5)
            scores = jnp.where(allowed, scores, -1e30)
            top = jnp.max(scores, axis=-1, keepdims=True)
            size = jnp.log(jnp.sum(jnp.exp(scores - top), axis=-1, keepdims=True)) + top
            share = jnp.exp(scores - size).astype(jnp.bfloat16)
            part = jnp.dot(
                share, v_heads[2 * quad + n // 2], preferred_element_type=jnp.float32
            )
            part = jnp.concatenate([part, jnp.zeros((rows, QUAD - 128), jnp.float32)], axis=1)
            total = total + (part if n == 0 else pltpu.roll(part, n * HEAD, 1))
            out_lse[...] += jnp.where(spot == 4 * quad + n, size, 0.0)
        mixed[:, quad * QUAD : (quad + 1) * QUAD] = total.astype(jnp.bfloat16)
        span = slice(quad * QUAD, (quad + 1) * QUAD)
        out_o[span, :] = total.T.astype(jnp.bfloat16)

    def attended():
        leave(out_o, turned_o)
        leave(out_lse, lse)

    def output():
        load = fetch(1, 0, 0, w_out)
        load.wait()
        for n in range(model // TILE):
            span = pl.ds(n * TILE, TILE)
            field[:, span] += jnp.dot(
                mixed[...], w_out[:, span], preferred_element_type=jnp.float32
            )
        leave(field, middle)
        norm(1)
        out_m[...] = normed[...].astype(jnp.float32).T.astype(jnp.bfloat16)
        leave(out_m, turned_m)

    hidden_units = gate_up.shape[1] // 2
    pairs = {}

    def fetch_pair(n):
        pairs[n] = [
            fetch(2, 2 * (n % 2) + k, k * hidden_units + n * TILE, tiles.at[n % 2, k])
            for k in range(2)
        ]

    def feed(n, last):
        if n not in pairs:
            fetch_pair(n)
        if n < last:
            fetch_pair(n + 1)
        for load in pairs[n]:
            load.wait()
        slot = n % 2
        if n >= 2:
            for copy in stored[n - 2]:
                copy.wait()
        both = []
        for k in range(2):
            value = jnp.dot(normed[...], tiles[slot, k], preferred_element_type=jnp.float32)
            pre[slot, k] = value
            both.append(value)
        gate, upper = both
        hidden = gate * jax.nn.sigmoid(gate) * upper
        out_h[n * TILE : (n + 1) * TILE, :] = hidden.T.astype(jnp.bfloat16)
        stored[n] = []
        for k in range(2):
            copy = pltpu.make_async_copy(
                pre.at[slot, k],
                gate_up.at[:, pl.ds(k * hidden_units + n * TILE, TILE)],
                tile_sem.at[4 + 2 * slot + k],
            )
            copy.start()
            stored[n].append(copy)

    stored = {}
    half = hidden_units // TILE // 2
    work = {
        "begin": begin,
        "project": lambda: (projections(), rope()),
        "attend0": lambda: [attend(n) for n in range(2)],
        "attend1": lambda: ([attend(n) for n in range(2, 4)], attended()),
        "output": output,
        "feed0": lambda: [feed(n, half - 1) for n in range(half)],
        "feed1": lambda: [feed(n, 2 * half - 1) for n in range(half, 2 * half)],
    }
    phases = [Item.first, Item.relay, Item.pass_on, Item.across, Item.complete]
    for time in range(len(items) + len(phases) - 1):
        for late, phase in enumerate(phases):
            if 0 <= time - late < len(items):
                phase(items[time - late])
        for name in stages.get(time, ()):
            work[name]()
    leave(out_h, turned_h)
    for item in items:
        item.finish()
    for copies in list(stored.values())[-2:]:
        for copy in copies:
            copy.wait()
    for copy in leaving:
        copy.wait()


def gather_forward(n_shard, weights, gain, tokens, cosine, sine, mask):
    def single(weight, share):
        return round_to(weight.shape[0] // 2 * share, 16)

    qkv, out, gate_up, down = weights
    part = gate_up.shape[1] // 4
    rows, model = tokens.shape
    wide, hidden = gate_up.shape[1], gate_up.shape[1] // 2
    third = [single(weight, 0.333) for weight in weights]
    plan = [
        (0, 0, qkv.shape[1] // 2, third[0]),
        (0, qkv.shape[1] // 2, qkv.shape[1] // 2, third[0]),
        (1, 0, model, third[1]),
        (2, 0, part, third[2]),
        (2, 2 * part, part, third[2]),
        (2, part, part, third[2]),
        (2, 3 * part, part, third[2]),
        (3, 0, model // 2, third[3]),
        (3, model // 2, model // 2, third[3]),
    ]
    stages = {
        0: ["begin"],
        5: ["project"],
        6: ["attend0"],
        7: ["attend1"],
        8: ["output", "feed0"],
        10: ["feed1"],
    }
    copies = 4 * (n_shard - 1)
    n = len(plan)
    anywhere = pl.BlockSpec(memory_space=pl.ANY)
    whole = pl.BlockSpec(memory_space=pltpu.VMEM)
    bf16, f32 = jnp.bfloat16, jnp.float32
    shape = jax.ShapeDtypeStruct
    heads = lambda count: pltpu.VMEM((count, rows, 128), bf16)
    return pl.pallas_call(
        functools.partial(forward_kernel, n_shard, plan, stages),
        out_shape=[shape((w.shape[0] * n_shard, w.shape[1]), w.dtype) for w in weights]
        + [
            shape((model, rows), bf16),
            shape((model, rows), bf16),
            shape((model, rows), bf16),
            shape((hidden, rows), bf16),
            shape((rows, qkv.shape[1]), bf16),
            shape((rows, 128), f32),
            shape((rows, model), f32),
            shape((rows, wide), f32),
            shape((n_shard,) + gain.shape, f32),
        ],
        in_specs=[anywhere] * 4 + [whole] * 5,
        out_specs=[anywhere] * 13,
        scratch_shapes=[pltpu.VMEM(w.shape, w.dtype) for w in weights]
        + [
            pltpu.VMEM((n_shard,) + gain.shape, f32),
            pltpu.VMEM((model, qkv.shape[1]), bf16),
            pltpu.VMEM((model, model), bf16),
            pltpu.VMEM((2, 2, model, TILE), bf16),
            pltpu.VMEM((rows, model), f32),
            pltpu.VMEM((rows, model), bf16),
            pltpu.VMEM((rows, qkv.shape[1]), f32),
            heads(HEADS),
            heads(KV_HEADS),
            heads(KV_HEADS),
            pltpu.VMEM((rows, model), bf16),
            pltpu.VMEM((model, rows), bf16),
            pltpu.VMEM((model, rows), bf16),
            pltpu.VMEM((model, rows), bf16),
            pltpu.VMEM((hidden, rows), bf16),
            pltpu.VMEM((rows, qkv.shape[1]), bf16),
            pltpu.VMEM((rows, 128), f32),
            pltpu.VMEM((2, 2, rows, TILE), f32),
            pltpu.SemaphoreType.DMA((n,)),
            pltpu.SemaphoreType.DMA((n,)),
            pltpu.SemaphoreType.DMA((n, copies)),
            pltpu.SemaphoreType.DMA((n, copies)),
            pltpu.SemaphoreType.DMA((n_shard - 1,)),
            pltpu.SemaphoreType.DMA((n_shard - 1,)),
            pltpu.SemaphoreType.DMA((1,)),
            pltpu.SemaphoreType.DMA((8,)),
            pltpu.SemaphoreType.DMA((16,)),
        ],
        compiler_params=pltpu.CompilerParams(
            collective_id=1, has_side_effects=True, vmem_limit_bytes=66_000_000
        ),
        name="gather_forward",
    )(*weights, gain, tokens, cosine, sine, mask)


SLOTS = 5


class Pipe:
    def __init__(self, n_shard, n_replica, begin, count, block, deliver, bufs, sems):
        self.shard, self.replica = lax.axis_index("shard"), lax.axis_index("replica")
        chip = self.replica // 2
        self.inner = lax.rem(chip, 2) != lax.rem(chip // 2, 2)
        self.steps = n_shard.bit_length() - 1
        self.swaps = [6] + [1 << k for k in range(3, n_replica.bit_length() - 1)]
        self.begin, self.count, self.block, self.deliver = begin, count, block, deliver
        bufs = list(bufs)
        self.out = [bufs.pop(0) for _ in range(self.steps)]
        self.into = [bufs.pop(0) for _ in range(self.steps)]
        self.kept = [bufs.pop(0) for _ in range(max(1, self.steps - 1))]
        self.fold_out, self.fold_in, self.total = bufs.pop(0), bufs.pop(0), bufs.pop(0)
        self.swap_out = [bufs.pop(0) for _ in self.swaps]
        self.swap_in = [bufs.pop(0) for _ in self.swaps]
        self.final, self.across = bufs.pop(0), bufs.pop(0)
        self.send_sem, self.recv_sem, self.local_sem = sems
        self.last = self.steps + 2 + len(self.swaps)

    @staticmethod
    def scratch(n_shard, n_replica, rows, cols, dtype):
        steps = n_shard.bit_length() - 1
        swaps = n_replica.bit_length() - 3
        blocks = [n_shard >> (k + 1) for k in range(steps)]
        shapes = [pltpu.VMEM((SLOTS, b, rows, cols), dtype) for b in blocks * 2]
        shapes += [
            pltpu.VMEM((SLOTS, max(1, b // 2), rows, cols), jnp.float32)
            for b in blocks[: max(1, steps - 1)]
        ]
        one = (SLOTS, rows, cols)
        shapes += [pltpu.VMEM(one, dtype)] * 2 + [pltpu.VMEM(one, jnp.float32)]
        shapes += [pltpu.VMEM(one, dtype)] * (2 * swaps + 2)
        kinds = steps + swaps + 3
        return shapes, [
            pltpu.SemaphoreType.DMA((kinds, SLOTS)),
            pltpu.SemaphoreType.DMA((kinds, SLOTS)),
            pltpu.SemaphoreType.DMA((2, SLOTS)),
        ]

    def bit(self, chunk, step):
        return 1 << lax.rem(step + lax.rem(chunk, 2), self.steps)

    def mask(self, chunk, entry):
        found = 0
        for step in range(self.steps):
            if (entry >> step) & 1:
                found = found | self.bit(chunk, step)
        return found

    def copy(self, kind, slot, src, dst, device):
        return pltpu.make_async_remote_copy(
            src_ref=src.at[slot],
            dst_ref=dst.at[slot],
            send_sem=self.send_sem.at[kind, slot],
            recv_sem=self.recv_sem.at[kind, slot],
            device_id=device,
            device_id_type=MESH,
        )

    def halving(self, step, chunk, slot):
        device = {"shard": self.shard ^ self.bit(chunk, step)}
        return self.copy(step, slot, self.out[step], self.into[step], device)

    def folding(self, slot):
        return self.copy(
            self.steps, slot, self.fold_out, self.fold_in, {"replica": self.replica ^ 2}
        )

    def swapping(self, number, slot):
        device = {"replica": self.replica ^ self.swaps[number]}
        return self.copy(
            self.steps + 1 + number, slot, self.swap_out[number], self.swap_in[number], device
        )

    def unfolding(self, slot):
        kind = self.steps + 1 + len(self.swaps)
        return self.copy(kind, slot, self.final, self.final, {"replica": self.replica ^ 2})

    def crossing(self, slot):
        kind = self.steps + 2 + len(self.swaps)
        return self.copy(kind, slot, self.final, self.across, {"replica": self.replica ^ 1})

    def stage(self, number, chunk, slot):
        steps, swaps = self.steps, len(self.swaps)
        dtype = self.final.dtype
        if number == 0:
            for entry in range(1, 1 << steps, 2):
                self.out[0][slot, entry >> 1] = self.block(chunk, self.mask(chunk, entry)).astype(dtype)
            self.halving(0, chunk, slot).start()
        elif number <= steps:
            sums = []
            for entry in range(1 << (steps - number)):
                if number == 1:
                    sums.append(self.block(chunk, self.mask(chunk, 2 * entry)))
                else:
                    sums.append(self.kept[number - 2][slot, entry])
            self.halving(number - 1, chunk, slot).wait()
            for entry, value in enumerate(sums):
                value = value + self.into[number - 1][slot, entry].astype(jnp.float32)
                if number == steps:
                    @pl.when(self.inner)
                    def _(value=value):
                        self.total[slot] = value

                    @pl.when(jnp.logical_not(self.inner))
                    def _(value=value):
                        self.fold_out[slot] = value.astype(dtype)
                        self.folding(slot).start()
                elif entry & 1:
                    self.out[number][slot, entry >> 1] = value.astype(dtype)
                else:
                    self.kept[number - 1][slot, entry >> 1] = value
            if number < steps:
                self.halving(number, chunk, slot).start()
        elif number == steps + 1:
            @pl.when(self.inner)
            def _():
                self.folding(slot).wait_recv()
                value = self.total[slot] + self.fold_in[slot].astype(jnp.float32)
                self.swap_out[0][slot] = value.astype(dtype)
                self.swapping(0, slot).start()

            @pl.when(jnp.logical_not(self.inner))
            def _():
                self.folding(slot).wait_send()
        elif number <= steps + 1 + swaps:
            @pl.when(self.inner)
            def _():
                done = number - steps - 2
                self.swapping(done, slot).wait()
                value = self.swap_out[done][slot].astype(jnp.float32) + self.swap_in[done][
                    slot
                ].astype(jnp.float32)
                if done + 1 < swaps:
                    self.swap_out[done + 1][slot] = value.astype(dtype)
                    self.swapping(done + 1, slot).start()
                else:
                    self.final[slot] = value.astype(dtype)
                    self.unfolding(slot).start()
        elif number == self.last:
            @pl.when(jnp.logical_not(self.inner))
            def _():
                self.unfolding(slot).wait_recv()

            self.crossing(slot).start()
            self.deliver(chunk, 0, self.final.at[slot], self.local_sem.at[0, slot], True)
        else:
            @pl.when(self.inner)
            def _():
                self.unfolding(slot).wait_send()

            self.crossing(slot).wait()
            self.deliver(chunk, 1, self.across.at[slot], self.local_sem.at[1, slot], True)
            self.deliver(chunk, 0, self.final.at[slot], self.local_sem.at[0, slot], False)
            self.deliver(chunk, 1, self.across.at[slot], self.local_sem.at[1, slot], False)

    def run(self, time):
        for number in range(self.last + 2):
            chunk = time - self.begin - number

            @pl.when((chunk >= 0) & (chunk < self.count))
            def _(number=number, chunk=chunk):
                self.stage(number, chunk, lax.rem(chunk, SLOTS))

    def length(self):
        return self.begin + self.count + self.last + 1


DEEP_COLS = 128
WIDE_COLS = 256


def reduce_kernel(n_shard, n_replica, halves, *refs):
    refs = list(refs)
    take = lambda n: [refs.pop(0) for _ in range(n)]
    lefts, rights, (gain_in,) = take(4), take(4), take(1)
    outs, (gain_out,) = take(4), take(1)
    deep_left, deep_right, wide_left, wide_right = take(4)
    load_sem, pass_send, pass_recv = take(3)
    n_bufs = (len(refs) - 9) // 3
    deep_bufs, deep_sems = take(n_bufs), take(3)
    wide_bufs, wide_sems = take(n_bufs), take(3)
    gain_bufs, gain_sems = take(n_bufs), take(3)
    shard, replica = lax.axis_index("shard"), lax.axis_index("replica")
    core = lax.rem(replica, 2)
    rows = lefts[0].shape[1]
    model = lefts[1].shape[0]
    deep_rows, wide_rows = outs[0].shape[0], outs[1].shape[0]

    place_left = [deep_left] + [wide_left.at[pl.ds(k * model, model)] for k in range(3)]
    starts = [0, 0, halves[1], halves[1] + halves[2]]
    place_right = [
        (deep_right if k == 0 else wide_right).at[:, pl.ds(starts[k], halves[k])] for k in range(4)
    ]
    loads, passes = [], []
    greet(
        [{"shard": shard ^ (1 << k)} for k in range(n_shard.bit_length() - 1)]
        + [{"replica": replica ^ mask} for mask in [1, 2, 6]]
        + [{"replica": replica ^ (1 << k)} for k in range(3, n_replica.bit_length() - 1)]
    )
    for k in range(4):
        mine = pl.ds(pl.multiple_of(core * halves[k], 128), halves[k])
        other = pl.ds(pl.multiple_of((1 - core) * halves[k], 128), halves[k])
        sources = [
            (lefts[k], place_left[k].at[:, pl.ds(0, rows)]),
            (rights[k].at[:, mine], place_right[k].at[pl.ds(0, rows)]),
        ]
        for n, (src, dst) in enumerate(sources):
            loads.append(pltpu.make_async_copy(src, dst, load_sem.at[2 * k + n]))
            loads[-1].start()
        sources = [
            (lefts[k], place_left[k].at[:, pl.ds(rows, rows)]),
            (rights[k].at[:, other], place_right[k].at[pl.ds(rows, rows)]),
        ]
        for n, (src, dst) in enumerate(sources):
            passes.append(
                pltpu.make_async_remote_copy(
                    src_ref=src,
                    dst_ref=dst,
                    send_sem=pass_send.at[2 * k + n],
                    recv_sem=pass_recv.at[2 * k + n],
                    device_id={"replica": replica ^ 1},
                    device_id_type=MESH,
                )
            )
            passes[-1].start()

    def arrived(first, end):
        for k in range(2 * first, 2 * end):
            loads[k].wait()
            passes[k].wait()

    def deep_block(chunk, mask):
        left = deep_left[pl.ds(pl.multiple_of((shard ^ mask) * deep_rows, 16), deep_rows), :]
        right = deep_right[:, pl.ds(pl.multiple_of(chunk * DEEP_COLS, 128), DEEP_COLS)]
        return jnp.dot(left, right, preferred_element_type=jnp.float32)

    bounds = [starts[k] // WIDE_COLS for k in (2, 3)]

    def wide_block(chunk, mask):
        weight = (chunk >= bounds[0]).astype(jnp.int32) + (chunk >= bounds[1]).astype(jnp.int32)
        start = weight * model + (shard ^ mask) * wide_rows
        left = wide_left[pl.ds(pl.multiple_of(start, 16), wide_rows), :]
        right = wide_right[:, pl.ds(pl.multiple_of(chunk * WIDE_COLS, 128), WIDE_COLS)]
        return jnp.dot(left, right, preferred_element_type=jnp.float32)

    def gain_block(chunk, mask):
        return gain_in[shard ^ mask]

    def put(out, start, size, src, sem, begin):
        copy = pltpu.make_async_copy(src, out.at[:, pl.ds(pl.multiple_of(start, 128), size)], sem)
        if begin:
            copy.start()
        else:
            copy.wait()

    def deep_deliver(chunk, side, src, sem, begin):
        half = jnp.where(side == 0, core, 1 - core) * halves[0]
        put(outs[0], half + chunk * DEEP_COLS, DEEP_COLS, src, sem, begin)

    def wide_deliver(chunk, side, src, sem, begin):
        edges = [0] + bounds + [wide_right.shape[1] // WIDE_COLS]
        half = core if side == 0 else 1 - core
        for k in range(3):
            @pl.when((chunk >= edges[k]) & (chunk < edges[k + 1]))
            def _(k=k):
                start = half * halves[k + 1] + (chunk - edges[k]) * WIDE_COLS
                put(outs[k + 1], start, WIDE_COLS, src, sem, begin)

    def gain_deliver(chunk, side, src, sem, begin):
        if side == 1 and begin:
            gain_out[...] = gain_pipe.final[0] + src[...]

    n_deep = halves[0] // DEEP_COLS
    n_wide = wide_right.shape[1] // WIDE_COLS
    size = (n_shard, n_replica)
    deep = Pipe(*size, 0, n_deep, deep_block, deep_deliver, deep_bufs, deep_sems)
    wide = Pipe(*size, n_deep, n_wide, wide_block, wide_deliver, wide_bufs, wide_sems)
    gain_pipe = Pipe(*size, 1, 1, gain_block, gain_deliver, gain_bufs, gain_sems)
    arrived(0, 1)

    def step(time, carry):
        @pl.when(time == n_deep)
        def _():
            arrived(1, 4)

        deep.run(time)
        gain_pipe.run(time)
        wide.run(time)
        return carry

    lax.fori_loop(0, wide.length(), step, 0)


def reduce_all(n_shard, n_replica, lefts, rights, gain_grads):
    rows = lefts[0].shape[1]
    halves = [right.shape[1] // 2 for right in rights]
    owned = [left.shape[0] // n_shard for left in lefts]
    model = lefts[1].shape[0]
    anywhere = pl.BlockSpec(memory_space=pl.ANY)
    whole = pl.BlockSpec(memory_space=pltpu.VMEM)
    size = (n_shard, n_replica)
    deep_bufs, deep_sems = Pipe.scratch(*size, owned[0], DEEP_COLS, jnp.bfloat16)
    wide_bufs, wide_sems = Pipe.scratch(*size, owned[1], WIDE_COLS, jnp.bfloat16)
    gain_bufs, gain_sems = Pipe.scratch(*size, *gain_grads.shape[1:], jnp.float32)
    return pl.pallas_call(
        functools.partial(reduce_kernel, n_shard, n_replica, halves),
        out_shape=[
            jax.ShapeDtypeStruct((own, right.shape[1]), jnp.bfloat16)
            for own, right in zip(owned, rights)
        ]
        + [jax.ShapeDtypeStruct(gain_grads.shape[1:], jnp.float32)],
        in_specs=[anywhere] * 8 + [whole],
        out_specs=[anywhere] * 4 + [whole],
        scratch_shapes=[
            pltpu.VMEM((lefts[0].shape[0], 2 * rows), jnp.bfloat16),
            pltpu.VMEM((2 * rows, halves[0]), jnp.bfloat16),
            pltpu.VMEM((3 * model, 2 * rows), jnp.bfloat16),
            pltpu.VMEM((2 * rows, sum(halves[1:])), jnp.bfloat16),
            pltpu.SemaphoreType.DMA((8,)),
            pltpu.SemaphoreType.DMA((8,)),
            pltpu.SemaphoreType.DMA((8,)),
            *deep_bufs,
            *deep_sems,
            *wide_bufs,
            *wide_sems,
            *gain_bufs,
            *gain_sems,
        ],
        compiler_params=pltpu.CompilerParams(
            collective_id=2, has_side_effects=True, vmem_limit_bytes=66_000_000
        ),
        name="reduce_gradients",
    )(*lefts, *rights, gain_grads)


def body(
    n_shard,
    n_replica,
    tokens,
    cotangent,
    seq_lengths,
    seq_device,
    seq_offsets,
    norm_attn,
    w_qkv,
    w_out,
    norm_mlp,
    w_gate_up,
    w_down,
):
    rows, model = tokens.shape
    w_qkv, w_out, w_gate_up, w_down = w_qkv[0], w_out[0], w_gate_up[0], w_down[0]
    owned_rows = w_qkv.shape[0]

    device = lax.axis_index(("shard", "replica"))
    segment, position = locate(device, seq_lengths, seq_device, seq_offsets, rows)
    live = (segment >= 0).astype(jnp.float32)[:, None]
    field = tokens.astype(jnp.float32)
    cosine, sine = rope_tables(position)
    allowed = mask_of(segment)

    (
        w_qkv,
        w_out,
        w_gate_up,
        w_down,
        normed_a_t,
        mixed_t,
        normed_m_t,
        hidden_t,
        roped,
        total,
        middle,
        pre,
        gains,
    ) = gather_forward(
        n_shard,
        (w_qkv, w_out, w_gate_up, w_down),
        jnp.concatenate([norm_attn, norm_mlp], axis=0).astype(jnp.float32),
        tokens,
        jnp.tile(cosine, (1, 4)),
        jnp.tile(sine, (1, 4)),
        allowed.astype(jnp.float32),
    )
    gains = gains.transpose(1, 0, 2).reshape(2, model)
    gain_attn, gain_mlp = gains[0], gains[1]
    per = HEADS // KV_HEADS
    queries_b = roped[:, : HEADS * HEAD].reshape(rows, HEADS, HEAD)
    keys_b = roped[:, HEADS * HEAD : (HEADS + KV_HEADS) * HEAD].reshape(rows, KV_HEADS, HEAD)
    values_b = roped[:, (HEADS + KV_HEADS) * HEAD :].reshape(rows, KV_HEADS, HEAD)
    total = total[:, :HEADS].T.reshape(KV_HEADS, per, rows, 1)
    scale_a, scale_m = rms_scale(field), rms_scale(middle)
    gate, upper = pre[:, :FF], pre[:, FF:]
    result = ((middle + contract_rows(hidden_t, w_down)) * live).astype(jnp.bfloat16)

    grad_field = cotangent.astype(jnp.float32) * live
    grad_last = grad_field.astype(jnp.bfloat16)
    grad_hidden = contract_cols(grad_last, w_down)
    grad_pre = jnp.concatenate(gate_back(grad_hidden, gate, upper), axis=1)
    grad_input, grad_gain_mlp = norm_back(
        contract_cols(grad_pre, w_gate_up), middle, scale_m, gain_mlp
    )
    grad_middle = grad_field + grad_input

    grad_branch = grad_middle.astype(jnp.bfloat16)
    grad_mixed = contract_cols(grad_branch, w_out).astype(jnp.bfloat16)
    grad_queries, grad_keys, grad_values = attend_backward(
        grad_mixed, queries_b, keys_b, values_b, total, allowed
    )
    grad_project = join_grads(grad_queries, grad_keys, grad_values, cosine, sine)
    grad_input, grad_gain_attn = norm_back(
        contract_cols(grad_project, w_qkv), field, scale_a, gain_attn
    )
    grad_tokens = grad_middle + grad_input

    gain_grads = jnp.stack([grad_gain_attn, grad_gain_mlp]).reshape(2, n_shard, owned_rows)
    gain_grads = jnp.pad(gain_grads.transpose(1, 0, 2), ((0, 0), (0, 6), (0, 0)))
    grad_down, grad_gate_up, grad_qkv, grad_out, gain_own = reduce_all(
        n_shard,
        n_replica,
        [hidden_t, normed_m_t, normed_a_t, mixed_t],
        [grad_last, grad_pre, grad_project, grad_branch],
        gain_grads,
    )
    grad_down, grad_gate_up, grad_qkv, grad_out = [
        grad.astype(jnp.float32) for grad in (grad_down, grad_gate_up, grad_qkv, grad_out)
    ]
    return (
        result,
        grad_tokens,
        gain_own[0:1],
        grad_qkv[None],
        grad_out[None],
        gain_own[1:2],
        grad_gate_up[None],
        grad_down[None],
    )


def solution(mesh):
    n_shard = mesh.shape["shard"]
    n_replica = mesh.shape["replica"]
    placed = (
        P(("shard", "replica"), None),
        P(("shard", "replica"), None),
        P(),
        P(),
        P(),
        P(None, "shard"),
        P(None, "shard", None),
        P(None, "shard", None),
        P(None, "shard"),
        P(None, "shard", None),
        P(None, "shard", None),
    )

    def run(*args):
        return body(n_shard, n_replica, *args)

    return jax.shard_map(
        run,
        mesh=mesh,
        in_specs=placed,
        out_specs=(
            P(("shard", "replica"), None),
            P(("shard", "replica"), None),
            P(None, "shard"),
            P(None, "shard", None),
            P(None, "shard", None),
            P(None, "shard"),
            P(None, "shard", None),
            P(None, "shard", None),
        ),
        check_vma=False,
    )
```

profile of v0, /device:TPU:0, one launch (start us, length us, event | category | flops | bytes accessed | tf_op | source)
XLA Modules:
  0.0 543.4 jit_solution(6102185428679621081)
XLA Ops:
  2.5 0.9 copy.55.refs_6_
  3.4 0.9 copy.56.refs_7_
  5.8 170.1 %gather_forward.1 = (bf16[1536,3072]{1,0:T(8,128)(2,1)}, bf16[1536,1536]{1,0:T(8,128)(2,1)}, bf16[1536,8192]{1,0:T(8,128)(2,1)}, bf16[4096,1536]{1,0:T(8,128)(2,...) custom-call(bf16[384,3072]{1,0:T(8,128)(2,1)} %bitcast.113, ...), custom_call_target="tpu_custom_call" | custom-call | tf_op jit(solution)/shard_map/gather_forward/pallas_call | solution.py:537
  176.1 10.8 %multiply_convert_fusion.1 = (bf16[256,4096]{1,0:T(8,128)(2,1)}, bf16[256,4096]{1,0:T(8,128)(2,1)}) fusion(f32[256,8192]{1,0:T(8,128)} %get-tuple-element.29, bf16[256,1536]{1,0:T(8,128)(2,1)S(1)} %fusion.23.refs_4_, bf16[4096,1536]{1,0:T(8,128)(2,1)} %get-tuple-element.28), kind=kOutput, calls=%fused_computation.11 | convolution fusion | flops 3234856960 | bytes 25952256 | tf_op jit(solution)/shard_map/dot_general | solution.py:64
  187.2 13.1 %multiply_reduce_fusion = (f32[1536]{0:T(1024)S(1)}, f32[256]{0:T(256)S(1)}, f32[256,1536]{1,0:T(8,128)S(1)}) fusion(f32[256,1536]{1,0:T(8,128)S(1)} %copy-done.1, f32[256]{0:T(256)S(1)} %add_rsqrt_fusion.1, f32[1536]{0:T(1024)S(1)} %mul.225, bf16[1536,8192]{1,0:T(8,128)(2,1)} %get-tuple-element.30, bf16[256,4096]{1,0:T(8,128)(2,1)} %get-tuple-element.55, ...), kind=kOutput, calls=%fused_computation.39 | convolution fusion | flops 6453196800 | bytes 32520192 | tf_op jit(solution)/shard_map/dot_general | solution.py:64
  200.3 1.7 fusion.40
  203.0 3.7 convolution_convert_fusion
  207.0 1.4 copy-done.16
  209.4 1.2 slice.48
  210.9 2.8 fusion.43
  214.2 3.8 fusion
  218.0 2.1 fusion.2
  221.7 1.2 pad_maximum_fusion.1
  222.9 3.0 copy.66
  226.0 3.0 copy.64
  229.0 1.3 mul.242
  230.3 3.0 copy.65
  233.3 3.6 subtract_convert_fusion
  238.8 4.2 fusion.27
  243.0 1.2 copy.70
  244.4 7.9 %fusion.21 = (f32[1536]{0:T(1024)S(1)}, f32[256]{0:T(256)S(1)}, f32[256,1536]{1,0:T(8,128)}) fusion(bf16[256,1536]{1,0:T(8,128)(2,1)S(1)} %copy-done.5, f32[256]{0:T(256)S(1)} %add_rsqrt_fusion, f32[1536]{0:T(1024)S(1)} %mul.252, bf16[1536,3072]{1,0:T(8,128)(2,1)} %get-tuple-element.35, bf16[256,768]{1,0:T(8,128)(2,1)S(1)} %copy.70, ...), kind=kOutput, calls=%fused_computation.34 | convolution fusion | flops 2423388416 | bytes 13383680 | tf_op jit(solution)/shard_map/dot_general | solution.py:64
  253.0 1.3 pad_maximum_fusion.2.refs_6_
  254.4 4.0 pad_maximum_fusion.refs_5_
  258.4 258.0 %reduce_gradients.1 = (bf16[1024,1536]{1,0:T(8,128)(2,1)}, bf16[384,8192]{1,0:T(8,128)(2,1)}, bf16[384,3072]{1,0:T(8,128)(2,1)}, bf16[384,1536]{1,0:T(8,128)(2,1)}, f32[8,384]{1,0:T(8,128)}) custom-call(bf16[4096,256]{1,0:T(8,128)(2,1)} %get-tuple-element.27.refs_0_, bf16[1536,256]{1,0:T(8,128)(2,1)} %get-tuple-element.36.refs_1_, ...), custom_call_target="tpu_custom_call" | custom-call | tf_op jit(solution)/shard_map/reduce_gradients/pallas_call | solution.py:898
  516.4 9.3 %bitcast_convert_fusion = f32[1,384,8192]{2,1,0:T(8,128)} fusion(bf16[384,8192]{1,0:T(8,128)(2,1)} %get-tuple-element.42), kind=kLoop, calls=%fused_computation | loop fusion | flops 3145728 | bytes 18874368 | tf_op jit(solution)/shard_map/broadcast_in_dim | solution.py:1028
  525.7 4.1 bitcast_convert_fusion.1
  529.8 3.0 bitcast_convert_fusion.2
  532.8 1.7 bitcast_convert_fusion.3
  534.5 1.4 fusion.42
  535.9 1.6 fusion.20
  537.6 1.1 copy-done.4
  538.7 4.3 fusion.6
  (101 shorter events, 11.0 us)
Async XLA Ops:
  0.6 4.5 copy-start.26
  0.6 4.5 copy-start.25
  5.8 170.1 %copy-start.10 = (bf16[256,1536]{1,0:T(8,128)(2,1)S(1)}, bf16[256,1536]{1,0:T(8,128)(2,1)}, u32[]{:S(2)}) copy-start(bf16[256,1536]{1,0:T(8,128)(2,1)} %param.12) | copy-start | bytes 2359300
  176.1 10.8 %copy-start.11 = (bf16[256,1536]{1,0:T(8,128)(2,1)}, bf16[256,1536]{1,0:T(8,128)(2,1)S(1)}, u32[]{:S(2)}) copy-start(bf16[256,1536]{1,0:T(8,128)(2,1)S(1)} %fusion.23.refs_4_) | copy-start | bytes 2359300
  176.1 10.8 %copy-start.1 = (f32[256,1536]{1,0:T(8,128)S(1)}, f32[256,1536]{1,0:T(8,128)}, u32[]{:S(2)}) copy-start(f32[256,1536]{1,0:T(8,128)} %get-tuple-element.26) | copy-start | bytes 4718596
  176.1 11.0 %copy-start.24 = (f32[4,2,384]{2,1,0:T(2,128)S(1)}, f32[4,2,384]{2,1,0:T(2,128)}, u32[]{:S(2)}) copy-start(f32[4,2,384]{2,1,0:T(2,128)} %get-tuple-element.31) | copy-start | bytes 36868
  202.1 0.9 copy-start.7
  206.7 1.7 copy-start.16
  207.0 7.1 %copy-start.8 = (bf16[256,1536]{0,1:T(8,128)(2,1)}, bf16[256,1536]{0,1:T(8,128)(2,1)S(1)}, u32[]{:S(2)}) copy-start(bf16[256,1536]{0,1:T(8,128)(2,1)S(1)} %copy.62) | copy-start | bytes 2359300
  210.8 2.8 copy-start.17
  210.9 3.0 copy-start.23
  210.9 3.1 copy-start.22
  214.1 3.8 copy-start.20
  214.1 3.8 copy-start
  220.5 1.2 copy-start.3
  237.7 1.1 copy-start.9
  237.7 1.1 copy-start.21
  238.8 5.3 copy-start.5
  238.8 5.6 %copy-start.13 = (bf16[256,1536]{1,0:T(8,128)(2,1)S(1)}, bf16[256,1536]{1,0:T(8,128)(2,1)}, u32[]{:S(2)}) copy-start(bf16[256,1536]{1,0:T(8,128)(2,1)} %subtract_convert_fusion) | copy-start | bytes 2359300
  252.4 2.0 copy-start.15
  516.4 9.3 %copy-start.12 = (bf16[1024,1536]{1,0:T(8,128)(2,1)S(1)}, bf16[1024,1536]{1,0:T(8,128)(2,1)}, u32[]{:S(2)}) copy-start(bf16[1024,1536]{1,0:T(8,128)(2,1)} %get-tuple-element.43) | copy-start | bytes 9437188
  516.4 13.4 %copy-start.14 = (bf16[384,3072]{1,0:T(8,128)(2,1)S(1)}, bf16[384,3072]{1,0:T(8,128)(2,1)}, u32[]{:S(2)}) copy-start(bf16[384,3072]{1,0:T(8,128)(2,1)} %get-tuple-element.40) | copy-start | bytes 7077892
  525.7 11.8 %slice-start = ((s8[12582912]{0:T(1024)(128)(4,1)}), s8[4194304]{0:T(1024)(128)(4,1)S(1)}, s32[]{:S(2)}) async-start(s8[12582912]{0:T(1024)(128)(4,1)} %bitcast.100), calls=%async_computation | async-start | bytes 8388608
  525.7 11.8 %slice-start.1 = ((s8[12582912]{0:T(1024)(128)(4,1)}), s8[4194304]{0:T(1024)(128)(4,1)S(1)}, s32[]{:S(2)}) async-start(s8[12582912]{0:T(1024)(128)(4,1)} %bitcast.100), calls=%async_computation.1 | async-start | bytes 8388608
  529.8 3.0 copy-start.19
  529.8 6.1 %copy-start.6 = (f32[256,1536]{1,0:T(8,128)S(1)}, f32[256,1536]{1,0:T(8,128)}, u32[]{:S(2)}) copy-start(f32[256,1536]{1,0:T(8,128)} %get-tuple-element.53) | copy-start | bytes 4718596
  529.8 6.1 %copy-start.18 = (f32[256,1536]{1,0:T(8,128)S(1)}, f32[256,1536]{1,0:T(8,128)}, u32[]{:S(2)}) copy-start(f32[256,1536]{1,0:T(8,128)} %get-tuple-element.79) | copy-start | bytes 4718596
  532.8 4.8 slice-start.2
  535.9 1.6 copy-start.2
  535.9 2.8 copy-start.4
where the time goes:
time: 553 us; the launch traced here: 543 us
  Pallas kernels  428 us (77%)
  matrix products  51.9 us (9%)
  other arithmetic  38 us (7%)
  local copies, waits for them, and re-layouts  23.9 us (4%)
    pallas_call x1, Pallas kernels, reduce_all(): pl.pallas_call(functools.partial(reduce_kernel, n_shard, n_replica, halve...  258 us
    pallas_call x1, Pallas kernels, gather_forward(): pl.pallas_call(functools.partial(forward_kernel, n_shard, plan, stages),...  170 us
    dot_general x4, matrix products, contract_cols(): lax.dot_general(left, right, (((1,), (1,)), ((), ())), preferred_element_...  35.6 us

commit v1 on v0

--- a/solution.py
+++ b/solution.py
@@ -15,15 +15,6 @@
 
 epsilon = 1e-05
 rope_base = 100000.0
-
-
-def rms_scale(field):
-    return lax.rsqrt(jnp.mean(field * field, axis=-1, keepdims=True) + epsilon)
-
-
-def rotate(field):
-    half = field.shape[-1] // 2
-    return jnp.concatenate([-field[..., half:], field[..., :half]], axis=-1)
 
 
 def rope_tables(position):
@@ -58,73 +49,6 @@
     return lax.dot_general(
         left, right, (((0,), (0,)), ((), ())), preferred_element_type=jnp.float32
     )
-
-
-def contract_cols(left, right):
-    return lax.dot_general(
-        left, right, (((1,), (1,)), ((), ())), preferred_element_type=jnp.float32
-    )
-
-
-def norm_back(grad_normed, field, scale, gain):
-    normed = field * scale
-    grad_gain = jnp.sum(grad_normed * normed, axis=0)
-    inner = grad_normed * gain[None, :]
-    grad_field = scale * (inner - normed * jnp.mean(inner * normed, axis=-1, keepdims=True))
-    return (grad_field, grad_gain)
-
-
-def join_grads(grad_queries, grad_keys, grad_values, cosine, sine):
-    rows = grad_queries.shape[0]
-    grad_queries = grad_queries * cosine[:, None, :] - rotate(grad_queries * sine[:, None, :])
-    grad_keys = grad_keys * cosine[:, None, :] - rotate(grad_keys * sine[:, None, :])
-    return jnp.concatenate(
-        [
-            grad_queries.reshape(rows, -1),
-            grad_keys.reshape(rows, -1),
-            grad_values.reshape(rows, -1),
-        ],
-        axis=1,
-    ).astype(jnp.bfloat16)
-
-
-def attention_scores(queries_b, keys_b, allowed):
-    rows = queries_b.shape[0]
-    kv_count = keys_b.shape[1]
-    grouped = queries_b.reshape(rows, kv_count, queries_b.shape[1] // kv_count, HEAD)
-    scores = jnp.einsum(
-        "qkgd,pkd->kgqp", grouped, keys_b, preferred_element_type=jnp.float32
-    ) * HEAD ** (-0.5)
-    return jnp.where(allowed, scores, -1e30)
-
-
-def attend_backward(grad_mixed_b, queries_b, keys_b, values_b, total, allowed):
-    rows = queries_b.shape[0]
-    q_heads = queries_b.shape[1]
-    kv_count = keys_b.shape[1]
-    per = q_heads // kv_count
-    factor = HEAD ** (-0.5)
-    grad_mixed = grad_mixed_b.reshape(rows, kv_count, per, HEAD)
-    weights = jnp.exp(attention_scores(queries_b, keys_b, allowed) - total)
-    weights_b = weights.astype(jnp.bfloat16)
-    grad_values = jnp.einsum(
-        "kgqp,qkgd->pkd", weights_b, grad_mixed, preferred_element_type=jnp.float32
-    )
-    grad_weights = jnp.einsum(
-        "qkgd,pkd->kgqp", grad_mixed, values_b, preferred_element_type=jnp.float32
-    )
-    grad_scores = weights * (grad_weights - jnp.sum(weights * grad_weights, axis=-1, keepdims=True))
-    grad_scores_b = grad_scores.astype(jnp.bfloat16)
-    grouped = queries_b.reshape(rows, kv_count, per, HEAD)
-    grad_queries = jnp.einsum(
-        "kgqp,pkd->qkgd", grad_scores_b, keys_b, preferred_element_type=jnp.float32
-    )
-    grad_queries = grad_queries.reshape(rows, q_heads, HEAD) * factor
-    grad_keys = (
-        jnp.einsum("kgqp,qkgd->pkd", grad_scores_b, grouped, preferred_element_type=jnp.float32)
-        * factor
-    )
-    return (grad_queries, grad_keys, grad_values)
 
 
 def gate_back(grad_hidden, gate, upper):
@@ -286,10 +210,11 @@
     take = lambda n: [refs.pop(0) for _ in range(n)]
     weights, (gain, tokens, cosine, sine, mask) = take(4), take(5)
     fulls = take(4)
-    turned_a, turned_o, turned_m, turned_h, roped, lse, middle, gate_up, gains = take(9)
+    turned_a, turned_o, turned_m, turned_h, lse, middle, gate_up, gains = take(8)
+    heads_out = take(3)
     owns, (gain_all, w_qkv, w_out, tiles) = take(4), take(4)
     field, normed, project, q_heads, k_heads, v_heads, mixed = take(7)
-    out_a, out_o, out_m, out_h, out_roped, out_lse, pre = take(7)
+    out_a, out_o, out_m, out_h, out_lse, out_gain, pre = take(7)
     load_sem, local_sem, send_sem, recv_sem, gain_send, gain_recv, gain_sem, tile_sem, out_sem = take(9)
     shard, replica = lax.axis_index("shard"), lax.axis_index("replica")
     rows, model = tokens.shape
@@ -338,7 +263,7 @@
         value = scaled_rows(field[...])
         for other in range(n_shard):
             span = slice(other * owned, (other + 1) * owned)
-            normed[:, span] = (value[:, span] * gain_all[other, row : row + 1, :]).astype(jnp.bfloat16)
+            normed[:, span] = (value[:, span] * out_gain[row : row + 1, span]).astype(jnp.bfloat16)
 
     def fetch(weight, index, start, dst):
         copy = pltpu.make_async_copy(
@@ -351,7 +276,9 @@
         gain_own.wait()
         for other in range(1, n_shard):
             gain_copy(other, shard ^ other).wait()
-        leave(gain_all, gains)
+        for other in range(n_shard):
+            out_gain[:, other * owned : (other + 1) * owned] = gain_all[other]
+        leave(out_gain, gains)
         field[...] = tokens[...].astype(jnp.float32)
         norm(0)
         out_a[...] = normed[...].astype(jnp.float32).T.astype(jnp.bfloat16)
@@ -384,12 +311,12 @@
                     pltpu.roll(value, HEAD // 2, 1),
                 )
                 value = value * cosine[...] + turned * sine[...]
-            out_roped[:, span] = value.astype(jnp.bfloat16)
             base = [0, 4, 8, 12, 0, 4, 0, 4][quad]
             for n in range(4):
                 moved = value if n == 0 else pltpu.roll(value, QUAD - n * HEAD, 1)
                 heads[base + n] = jnp.where(in_head, moved[:, :128], 0.0).astype(jnp.bfloat16)
-        leave(out_roped, roped)
+        for src, dst in zip((q_heads, k_heads, v_heads), heads_out):
+            leave(src, dst)
         out_lse[...] = jnp.zeros_like(out_lse)
 
     def attend(quad):
@@ -542,14 +469,14 @@
             shape((model, rows), bf16),
             shape((model, rows), bf16),
             shape((hidden, rows), bf16),
-            shape((rows, qkv.shape[1]), bf16),
             shape((rows, 128), f32),
             shape((rows, model), f32),
             shape((rows, wide), f32),
-            shape((n_shard,) + gain.shape, f32),
-        ],
+            shape((2, model), f32),
+        ]
+        + [shape((count, rows, 128), bf16) for count in (HEADS, KV_HEADS, KV_HEADS)],
         in_specs=[anywhere] * 4 + [whole] * 5,
-        out_specs=[anywhere] * 13,
+        out_specs=[anywhere] * 15,
         scratch_shapes=[pltpu.VMEM(w.shape, w.dtype) for w in weights]
         + [
             pltpu.VMEM((n_shard,) + gain.shape, f32),
@@ -567,8 +494,8 @@
             pltpu.VMEM((model, rows), bf16),
             pltpu.VMEM((model, rows), bf16),
             pltpu.VMEM((hidden, rows), bf16),
-            pltpu.VMEM((rows, qkv.shape[1]), bf16),
             pltpu.VMEM((rows, 128), f32),
+            pltpu.VMEM((2, model), f32),
             pltpu.VMEM((2, 2, rows, TILE), f32),
             pltpu.SemaphoreType.DMA((n,)),
             pltpu.SemaphoreType.DMA((n,)),
@@ -602,8 +529,9 @@
         self.out = [bufs.pop(0) for _ in range(self.steps)]
         self.into = [bufs.pop(0) for _ in range(self.steps)]
         self.kept = [bufs.pop(0) for _ in range(max(1, self.steps - 1))]
-        self.fold_out, self.fold_in, self.total = bufs.pop(0), bufs.pop(0), bufs.pop(0)
+        self.fold_in = bufs.pop(0)
         self.swap_out = [bufs.pop(0) for _ in self.swaps]
+        self.fold_out = self.swap_out[0]
         self.swap_in = [bufs.pop(0) for _ in self.swaps]
         self.final, self.across = bufs.pop(0), bufs.pop(0)
         self.send_sem, self.recv_sem, self.local_sem = sems
@@ -620,8 +548,7 @@
             for b in blocks[: max(1, steps - 1)]
         ]
         one = (SLOTS, rows, cols)
-        shapes += [pltpu.VMEM(one, dtype)] * 2 + [pltpu.VMEM(one, jnp.float32)]
-        shapes += [pltpu.VMEM(one, dtype)] * (2 * swaps + 2)
+        shapes += [pltpu.VMEM(one, dtype)] * (2 * swaps + 3)
         kinds = steps + swaps + 3
         return shapes, [
             pltpu.SemaphoreType.DMA((kinds, SLOTS)),
@@ -692,7 +619,7 @@
                 if number == steps:
                     @pl.when(self.inner)
                     def _(value=value):
-                        self.total[slot] = value
+                        self.kept[-1][slot, 0] = value
 
                     @pl.when(jnp.logical_not(self.inner))
                     def _(value=value):
@@ -708,7 +635,7 @@
             @pl.when(self.inner)
             def _():
                 self.folding(slot).wait_recv()
-                value = self.total[slot] + self.fold_in[slot].astype(jnp.float32)
+                value = self.kept[-1][slot, 0] + self.fold_in[slot].astype(jnp.float32)
                 self.swap_out[0][slot] = value.astype(dtype)
                 self.swapping(0, slot).start()
 
@@ -760,158 +687,428 @@
 
 DEEP_COLS = 128
 WIDE_COLS = 256
-
-
-def reduce_kernel(n_shard, n_replica, halves, *refs):
+EARLY = 16
+
+
+def times_rows(left, right):
+    return lax.dot_general(
+        left, right, (((0,), (0,)), ((), ())), preferred_element_type=jnp.float32
+    )
+
+
+def times_cols(left, right):
+    return lax.dot_general(
+        left, right, (((1,), (1,)), ((), ())), preferred_element_type=jnp.float32
+    )
+
+
+def backward_kernel(n_shard, n_replica, *refs):
     refs = list(refs)
     take = lambda n: [refs.pop(0) for _ in range(n)]
-    lefts, rights, (gain_in,) = take(4), take(4), take(1)
-    outs, (gain_out,) = take(4), take(1)
-    deep_left, deep_right, wide_left, wide_right = take(4)
-    load_sem, pass_send, pass_recv = take(3)
+    lefts, (w_down, w_gate_up, w_out, w_qkv, pre) = take(4), take(5)
+    heads_in, middle_in = take(3), take(1)[0]
+    grad_last, tokens, gain, lse, cosine, sine, mask = take(7)
+    outs, (gain_out, grad_tokens) = take(4), take(2)
+    deep_left, deep_right, wide_left, wide_right, other_right = take(5)
+    tile_down, tile_up, tile_pre, tile_out = take(4)
+    q_heads, k_heads, v_heads, middle, grad_middle, total, branch, joined, parts, gain_in = take(10)
+    load_sem, pass_send, pass_recv, tile_send, tile_recv, tile_sem, head_sem, late_sem = take(8)
     n_bufs = (len(refs) - 9) // 3
     deep_bufs, deep_sems = take(n_bufs), take(3)
     wide_bufs, wide_sems = take(n_bufs), take(3)
     gain_bufs, gain_sems = take(n_bufs), take(3)
     shard, replica = lax.axis_index("shard"), lax.axis_index("replica")
     core = lax.rem(replica, 2)
-    rows = lefts[0].shape[1]
-    model = lefts[1].shape[0]
-    deep_rows, wide_rows = outs[0].shape[0], outs[1].shape[0]
-
-    place_left = [deep_left] + [wide_left.at[pl.ds(k * model, model)] for k in range(3)]
-    starts = [0, 0, halves[1], halves[1] + halves[2]]
-    place_right = [
-        (deep_right if k == 0 else wide_right).at[:, pl.ds(starts[k], halves[k])] for k in range(4)
-    ]
-    loads, passes = [], []
+    rows, model = grad_last.shape
+    hidden = w_down.shape[0]
+    wide = w_qkv.shape[1]
+    deep_rows, wide_rows = outs[0].shape[0] // 2, outs[1].shape[0]
+    halves = [model // 2, hidden, model // 2, wide // 2]
+    starts = [0, 0, hidden, hidden + model // 2]
+    n_deep = 2 * halves[0] // DEEP_COLS
+    edges = [start // WIDE_COLS for start in starts[1:]] + [wide_right.shape[1] // WIDE_COLS]
+    tile = hidden // EARLY
+    twin = {"replica": replica ^ 1}
+
     greet(
         [{"shard": shard ^ (1 << k)} for k in range(n_shard.bit_length() - 1)]
-        + [{"replica": replica ^ mask} for mask in [1, 2, 6]]
+        + [{"replica": replica ^ other} for other in [1, 2, 6]]
         + [{"replica": replica ^ (1 << k)} for k in range(3, n_replica.bit_length() - 1)]
     )
+
+    def pass_over(src, dst, sems, index):
+        return pltpu.make_async_remote_copy(
+            src_ref=src,
+            dst_ref=dst,
+            send_sem=sems[0].at[index],
+            recv_sem=sems[1].at[index],
+            device_id=twin,
+            device_id_type=MESH,
+        )
+
+    def half_of(which, side):
+        return pl.ds(pl.multiple_of(side * halves[which], 128), halves[which])
+
+    place_left = [deep_left] + [wide_left.at[pl.ds(k * model, model)] for k in range(3)]
+    loads, passes = [], []
     for k in range(4):
-        mine = pl.ds(pl.multiple_of(core * halves[k], 128), halves[k])
-        other = pl.ds(pl.multiple_of((1 - core) * halves[k], 128), halves[k])
-        sources = [
-            (lefts[k], place_left[k].at[:, pl.ds(0, rows)]),
-            (rights[k].at[:, mine], place_right[k].at[pl.ds(0, rows)]),
-        ]
-        for n, (src, dst) in enumerate(sources):
-            loads.append(pltpu.make_async_copy(src, dst, load_sem.at[2 * k + n]))
-            loads[-1].start()
-        sources = [
-            (lefts[k], place_left[k].at[:, pl.ds(rows, rows)]),
-            (rights[k].at[:, other], place_right[k].at[pl.ds(rows, rows)]),
-        ]
-        for n, (src, dst) in enumerate(sources):
+        loads.append(
+            pltpu.make_async_copy(lefts[k], place_left[k].at[:, pl.ds(0, rows)], load_sem.at[k])
+        )
+        passes.append(
+            pass_over(lefts[k], place_left[k].at[:, pl.ds(rows, rows)], (pass_send, pass_recv), k)
+        )
+        if k == 0:
             passes.append(
-                pltpu.make_async_remote_copy(
-                    src_ref=src,
-                    dst_ref=dst,
-                    send_sem=pass_send.at[2 * k + n],
-                    recv_sem=pass_recv.at[2 * k + n],
-                    device_id={"replica": replica ^ 1},
-                    device_id_type=MESH,
+                pass_over(
+                    grad_last.at[:, half_of(0, 1 - core)],
+                    deep_right.at[pl.ds(rows, rows)],
+                    (pass_send, pass_recv),
+                    4,
                 )
             )
-            passes[-1].start()
-
-    def arrived(first, end):
-        for k in range(2 * first, 2 * end):
-            loads[k].wait()
-            passes[k].wait()
-
-    def deep_block(chunk, mask):
-        left = deep_left[pl.ds(pl.multiple_of((shard ^ mask) * deep_rows, 16), deep_rows), :]
-        right = deep_right[:, pl.ds(pl.multiple_of(chunk * DEEP_COLS, 128), DEEP_COLS)]
+    for copy in loads + passes:
+        copy.start()
+    late = [
+        pltpu.make_async_copy(src, dst, late_sem.at[n])
+        for n, (src, dst) in enumerate(
+            zip([*heads_in, middle_in], [q_heads, k_heads, v_heads, middle])
+        )
+    ]
+    for copy in late:
+        copy.start()
+    deep_right[pl.ds(0, rows), :] = grad_last[:, half_of(0, core)]
+    total[...] = jnp.zeros_like(total)
+    gain_in[...] = jnp.zeros_like(gain_in)
+    tile_out[...] = jnp.zeros_like(tile_out)
+
+    def tile_copies(n, slot):
+        start = pl.multiple_of(n * tile, tile)
+        cols = [pl.ds(start, tile), pl.ds(pl.multiple_of(hidden + n * tile, tile), tile)]
+        pairs = [(w_down.at[cols[0]], tile_down.at[slot])]
+        for k in range(2):
+            pairs.append((w_gate_up.at[:, cols[k]], tile_up.at[slot, k]))
+            pairs.append((pre.at[:, cols[k]], tile_pre.at[slot, k]))
+        return [
+            pltpu.make_async_copy(src, dst, tile_sem.at[slot, k])
+            for k, (src, dst) in enumerate(pairs)
+        ]
+
+    def tile_pass(n):
+        span = pl.ds(pl.multiple_of(n * tile, tile), tile)
+        return pass_over(
+            other_right.at[lax.rem(n, 4)],
+            wide_right.at[pl.ds(rows, rows), span],
+            (tile_send, tile_recv),
+            n,
+        )
+
+    def hidden_tile(n):
+        slot = lax.rem(n, 2)
+
+        @pl.when(n + 1 < EARLY)
+        def _():
+            for copy in tile_copies(n + 1, 1 - slot):
+                copy.start()
+
+        for copy in tile_copies(n, slot):
+            copy.wait()
+        grad_hidden = times_cols(grad_last[...], tile_down[slot])
+        grad_gate, grad_upper = gate_back(grad_hidden, tile_pre[slot, 0], tile_pre[slot, 1])
+        span = pl.ds(pl.multiple_of(n * tile, tile), tile)
+        first = core == 0
+        wide_right[pl.ds(0, rows), span] = jnp.where(first, grad_gate, grad_upper)
+
+        @pl.when(n >= 4)
+        def _():
+            tile_pass(n - 4).wait_send()
+
+        other_right[lax.rem(n, 4)] = jnp.where(first, grad_upper, grad_gate)
+        tile_pass(n).start()
+        total[...] += times_cols(grad_gate, tile_up[slot, 0]) + times_cols(
+            grad_upper, tile_up[slot, 1]
+        )
+
+    def norm_gradient(field, row):
+        scale = lax.rsqrt(jnp.mean(field * field, axis=-1, keepdims=True) + epsilon)
+        normed = field * scale
+        grad = total[...]
+        sums = jnp.sum(grad * normed, axis=0, keepdims=True)
+        for other in range(n_shard):
+            gain_in[other, row : row + 1, :] = sums[:, other * wide_rows : (other + 1) * wide_rows]
+        inner = grad * gain[row : row + 1, :]
+        return scale * (inner - normed * jnp.mean(inner * normed, axis=-1, keepdims=True))
+
+    def share_right(which, source, index):
+        span = pl.ds(starts[which], halves[which])
+        wide_right[pl.ds(0, rows), span] = source[:, half_of(which, core)]
+        return pass_over(
+            source.at[:, half_of(which, 1 - core)],
+            wide_right.at[pl.ds(rows, rows), span],
+            (pass_send, pass_recv),
+            index,
+        )
+
+    def between():
+        for copy in late:
+            copy.wait()
+        for n in range(EARLY - 4, EARLY):
+            tile_pass(n).wait_send()
+        grad_middle[...] = grad_last[...].astype(jnp.float32) + norm_gradient(middle[...], 1)
+        branch[...] = grad_middle[...].astype(jnp.bfloat16)
+        share_right(2, branch, 5).start()
+        total[...] = jnp.zeros_like(total)
+        for copy in qkv_copies(0, 0):
+            copy.start()
+
+    per = HEADS // KV_HEADS
+
+    def head_copies(key_head, slot):
+        return [
+            pltpu.make_async_copy(
+                w_out.at[pl.ds(pl.multiple_of((per * key_head + n) * HEAD, 32), HEAD)],
+                tile_out.at[slot, n, pl.ds(0, HEAD)],
+                head_sem.at[slot, n],
+            )
+            for n in range(per)
+        ]
+
+    spot = lax.broadcasted_iota(jnp.int32, (rows, 128), 1)
+
+    def unrope(value):
+        moved = value * sine[...]
+        turned = jnp.where(
+            spot < HEAD // 2,
+            -pltpu.roll(moved, 128 - HEAD // 2, 1),
+            pltpu.roll(moved, HEAD // 2, 1),
+        )
+        return jnp.where(spot < HEAD, value * cosine[...] - turned, 0.0).astype(jnp.bfloat16)
+
+    def attention(key_head):
+        slot = lax.rem(key_head, 2)
+
+        @pl.when(key_head + 1 < KV_HEADS)
+        def _():
+            for copy in head_copies(key_head + 1, 1 - slot):
+                copy.start()
+
+        for copy in head_copies(key_head, slot):
+            copy.wait()
+        allowed = mask[...] > 0.5
+        factor = HEAD ** (-0.5)
+        key, value = k_heads[key_head], v_heads[key_head]
+        grad_key = jnp.zeros((rows, 128), jnp.float32)
+        grad_value = jnp.zeros((rows, 128), jnp.float32)
+        for n in range(per):
+            head = per * key_head + n
+            query = q_heads[head]
+            grad_mixed = times_cols(branch[...], tile_out[slot, n]).astype(jnp.bfloat16)
+            size = jnp.sum(jnp.where(spot == head, lse[...], 0.0), axis=-1, keepdims=True)
+            scores = jnp.where(allowed, times_cols(query, key) * factor, -1e30)
+            share = jnp.exp(scores - size)
+            grad_value = grad_value + times_rows(share.astype(jnp.bfloat16), grad_mixed)
+            grad_share = times_cols(grad_mixed, value)
+            inner = jnp.sum(share * grad_share, axis=-1, keepdims=True)
+            grad_scores = (share * (grad_share - inner)).astype(jnp.bfloat16)
+            grad_query = jnp.dot(grad_scores, key, preferred_element_type=jnp.float32) * factor
+            parts[head] = unrope(grad_query)
+            grad_key = grad_key + times_rows(grad_scores, query)
+        parts[HEADS + key_head] = unrope(grad_key * factor)
+        parts[HEADS + KV_HEADS + key_head] = grad_value.astype(jnp.bfloat16)
+
+    quad = 4 * HEAD
+
+    def join():
+        for group in range(wide // quad):
+            value = jnp.zeros((rows, quad), jnp.float32)
+            for n in range(4):
+                part = parts[4 * group + n].astype(jnp.float32)
+                part = jnp.concatenate([part, jnp.zeros((rows, quad - 128), jnp.float32)], axis=1)
+                value = value + (part if n == 0 else pltpu.roll(part, n * HEAD, 1))
+            joined[:, group * quad : (group + 1) * quad] = value.astype(jnp.bfloat16)
+        share_right(3, joined, 6).start()
+
+    n_last = wide // (2 * tile)
+
+    def qkv_copies(n, slot):
+        return [
+            pltpu.make_async_copy(
+                w_qkv.at[:, pl.ds(pl.multiple_of((2 * n + k) * tile, tile), tile)],
+                tile_up.at[slot, k],
+                tile_sem.at[slot, k],
+            )
+            for k in range(2)
+        ]
+
+    def input_tile(n):
+        slot = lax.rem(n, 2)
+
+        @pl.when(n + 1 < n_last)
+        def _():
+            for copy in qkv_copies(n + 1, 1 - slot):
+                copy.start()
+
+        for copy in qkv_copies(n, slot):
+            copy.wait()
+        for k in range(2):
+            span = pl.ds(pl.multiple_of((2 * n + k) * tile, tile), tile)
+            total[...] += times_cols(joined[:, span], tile_up[slot, k])
+
+    def end():
+        grad_tokens[...] = grad_middle[...] + norm_gradient(tokens[...].astype(jnp.float32), 0)
+
+    def deep_block(chunk, other):
+        start = (shard ^ other) * (2 * deep_rows) + (chunk // (n_deep // 2)) * deep_rows
+        left = deep_left[pl.ds(pl.multiple_of(start, 16), deep_rows), :]
+        cols = lax.rem(chunk, n_deep // 2) * DEEP_COLS
+        right = deep_right[:, pl.ds(pl.multiple_of(cols, 128), DEEP_COLS)]
         return jnp.dot(left, right, preferred_element_type=jnp.float32)
 
-    bounds = [starts[k] // WIDE_COLS for k in (2, 3)]
-
-    def wide_block(chunk, mask):
-        weight = (chunk >= bounds[0]).astype(jnp.int32) + (chunk >= bounds[1]).astype(jnp.int32)
-        start = weight * model + (shard ^ mask) * wide_rows
+    def wide_block(chunk, other):
+        weight = (chunk >= edges[1]).astype(jnp.int32) + (chunk >= edges[2]).astype(jnp.int32)
+        start = weight * model + (shard ^ other) * wide_rows
         left = wide_left[pl.ds(pl.multiple_of(start, 16), wide_rows), :]
         right = wide_right[:, pl.ds(pl.multiple_of(chunk * WIDE_COLS, 128), WIDE_COLS)]
         return jnp.dot(left, right, preferred_element_type=jnp.float32)
 
-    def gain_block(chunk, mask):
-        return gain_in[shard ^ mask]
-
-    def put(out, start, size, src, sem, begin):
-        copy = pltpu.make_async_copy(src, out.at[:, pl.ds(pl.multiple_of(start, 128), size)], sem)
+    def put(out, span, start, size, src, sem, begin):
+        copy = pltpu.make_async_copy(
+            src, out.at[span, pl.ds(pl.multiple_of(start, 128), size)], sem
+        )
         if begin:
             copy.start()
         else:
             copy.wait()
 
     def deep_deliver(chunk, side, src, sem, begin):
-        half = jnp.where(side == 0, core, 1 - core) * halves[0]
-        put(outs[0], half + chunk * DEEP_COLS, DEEP_COLS, src, sem, begin)
+        half = core if side == 0 else 1 - core
+        first = pl.multiple_of((chunk // (n_deep // 2)) * deep_rows, 16)
+        start = half * halves[0] + lax.rem(chunk, n_deep // 2) * DEEP_COLS
+        put(outs[0], pl.ds(first, deep_rows), start, DEEP_COLS, src, sem, begin)
 
     def wide_deliver(chunk, side, src, sem, begin):
-        edges = [0] + bounds + [wide_right.shape[1] // WIDE_COLS]
         half = core if side == 0 else 1 - core
         for k in range(3):
             @pl.when((chunk >= edges[k]) & (chunk < edges[k + 1]))
             def _(k=k):
                 start = half * halves[k + 1] + (chunk - edges[k]) * WIDE_COLS
-                put(outs[k + 1], start, WIDE_COLS, src, sem, begin)
+                put(outs[k + 1], slice(None), start, WIDE_COLS, src, sem, begin)
 
     def gain_deliver(chunk, side, src, sem, begin):
         if side == 1 and begin:
             gain_out[...] = gain_pipe.final[0] + src[...]
 
-    n_deep = halves[0] // DEEP_COLS
-    n_wide = wide_right.shape[1] // WIDE_COLS
+    between_at = EARLY
+    join_at = between_at + 1 + KV_HEADS
+    end_at = join_at + 1 + n_last
     size = (n_shard, n_replica)
     deep = Pipe(*size, 0, n_deep, deep_block, deep_deliver, deep_bufs, deep_sems)
-    wide = Pipe(*size, n_deep, n_wide, wide_block, wide_deliver, wide_bufs, wide_sems)
-    gain_pipe = Pipe(*size, 1, 1, gain_block, gain_deliver, gain_bufs, gain_sems)
-    arrived(0, 1)
+    wide_pipe = Pipe(
+        *size, n_deep, edges[3], wide_block, wide_deliver, wide_bufs, wide_sems
+    )
+    gain_pipe = Pipe(
+        *size, end_at + 1, 1, lambda chunk, other: gain_in[shard ^ other], gain_deliver, gain_bufs, gain_sems
+    )
+    for copy in tile_copies(0, 0):
+        copy.start()
+    for copy in head_copies(0, 0):
+        copy.start()
+    loads[0].wait()
+    passes[0].wait()
+    passes[1].wait()
 
     def step(time, carry):
+        def at(first, count, run):
+            @pl.when((time >= first) & (time < first + count))
+            def _():
+                run(time - first)
+
         @pl.when(time == n_deep)
         def _():
-            arrived(1, 4)
-
+            for k in range(1, 4):
+                loads[k].wait()
+                passes[k + 1].wait()
+
+        at(n_deep, EARLY, lambda n: tile_pass(n).wait_recv())
+        at(n_deep + edges[1], 1, lambda n: share_wait(2, branch, 5))
+        at(n_deep + edges[2], 1, lambda n: share_wait(3, joined, 6))
         deep.run(time)
+        wide_pipe.run(time)
         gain_pipe.run(time)
-        wide.run(time)
+        at(0, EARLY, hidden_tile)
+        at(between_at, 1, lambda n: between())
+        at(between_at + 1, KV_HEADS, attention)
+        at(join_at, 1, lambda n: join())
+        at(join_at + 1, n_last, input_tile)
+        at(end_at, 1, lambda n: end())
         return carry
 
-    lax.fori_loop(0, wide.length(), step, 0)
-
-
-def reduce_all(n_shard, n_replica, lefts, rights, gain_grads):
-    rows = lefts[0].shape[1]
-    halves = [right.shape[1] // 2 for right in rights]
-    owned = [left.shape[0] // n_shard for left in lefts]
-    model = lefts[1].shape[0]
+    def share_wait(which, source, index):
+        span = pl.ds(starts[which], halves[which])
+        pass_over(
+            source.at[:, half_of(which, 1 - core)],
+            wide_right.at[pl.ds(rows, rows), span],
+            (pass_send, pass_recv),
+            index,
+        ).wait()
+
+    lax.fori_loop(0, max(wide_pipe.length(), gain_pipe.length()), step, 0)
+
+
+def backward_all(n_shard, n_replica, lefts, weights, pre, heads, middle, small):
+    grad_last, tokens, gain, lse = small[:4]
+    rows, model = grad_last.shape
+    w_down, w_gate_up, w_out, w_qkv = weights
+    hidden, wide = w_down.shape[0], w_qkv.shape[1]
+    tile = hidden // EARLY
+    owned = [w.shape[0] // n_shard for w in weights]
     anywhere = pl.BlockSpec(memory_space=pl.ANY)
     whole = pl.BlockSpec(memory_space=pltpu.VMEM)
+    bf16, f32 = jnp.bfloat16, jnp.float32
     size = (n_shard, n_replica)
-    deep_bufs, deep_sems = Pipe.scratch(*size, owned[0], DEEP_COLS, jnp.bfloat16)
-    wide_bufs, wide_sems = Pipe.scratch(*size, owned[1], WIDE_COLS, jnp.bfloat16)
-    gain_bufs, gain_sems = Pipe.scratch(*size, *gain_grads.shape[1:], jnp.float32)
+    deep_bufs, deep_sems = Pipe.scratch(*size, owned[0] // 2, DEEP_COLS, bf16)
+    wide_bufs, wide_sems = Pipe.scratch(*size, owned[1], WIDE_COLS, bf16)
+    gain_bufs, gain_sems = Pipe.scratch(*size, 8, owned[1], f32)
+    dma = pltpu.SemaphoreType.DMA
     return pl.pallas_call(
-        functools.partial(reduce_kernel, n_shard, n_replica, halves),
+        functools.partial(backward_kernel, n_shard, n_replica),
         out_shape=[
-            jax.ShapeDtypeStruct((own, right.shape[1]), jnp.bfloat16)
-            for own, right in zip(owned, rights)
+            jax.ShapeDtypeStruct((own, w.shape[1]), bf16) for own, w in zip(owned, weights)
         ]
-        + [jax.ShapeDtypeStruct(gain_grads.shape[1:], jnp.float32)],
-        in_specs=[anywhere] * 8 + [whole],
-        out_specs=[anywhere] * 4 + [whole],
+        + [
+            jax.ShapeDtypeStruct((8, owned[1]), f32),
+            jax.ShapeDtypeStruct((rows, model), f32),
+        ],
+        in_specs=[anywhere] * 13 + [whole] * 7,
+        out_specs=[anywhere] * 4 + [whole] * 2,
         scratch_shapes=[
-            pltpu.VMEM((lefts[0].shape[0], 2 * rows), jnp.bfloat16),
-            pltpu.VMEM((2 * rows, halves[0]), jnp.bfloat16),
-            pltpu.VMEM((3 * model, 2 * rows), jnp.bfloat16),
-            pltpu.VMEM((2 * rows, sum(halves[1:])), jnp.bfloat16),
-            pltpu.SemaphoreType.DMA((8,)),
-            pltpu.SemaphoreType.DMA((8,)),
-            pltpu.SemaphoreType.DMA((8,)),
+            pltpu.VMEM((hidden, 2 * rows), bf16),
+            pltpu.VMEM((2 * rows, model // 2), bf16),
+            pltpu.VMEM((3 * model, 2 * rows), bf16),
+            pltpu.VMEM((2 * rows, hidden + model // 2 + wide // 2), bf16),
+            pltpu.VMEM((4, rows, tile), bf16),
+            pltpu.VMEM((2, tile, model), bf16),
+            pltpu.VMEM((2, 2, model, tile), bf16),
+            pltpu.VMEM((2, 2, rows, tile), f32),
+            pltpu.VMEM((2, HEADS // KV_HEADS, 128, model), bf16),
+            pltpu.VMEM((HEADS, rows, 128), bf16),
+            pltpu.VMEM((KV_HEADS, rows, 128), bf16),
+            pltpu.VMEM((KV_HEADS, rows, 128), bf16),
+            pltpu.VMEM((rows, model), f32),
+            pltpu.VMEM((rows, model), f32),
+            pltpu.VMEM((rows, model), f32),
+            pltpu.VMEM((rows, model), bf16),
+            pltpu.VMEM((rows, wide), bf16),
+            pltpu.VMEM((HEADS + 2 * KV_HEADS, rows, 128), bf16),
+            pltpu.VMEM((n_shard, 8, owned[1]), f32),
+            dma((4,)),
+            dma((7,)),
+            dma((7,)),
+            dma((EARLY,)),
+            dma((EARLY,)),
+            dma((2, 5)),
+            dma((2, HEADS // KV_HEADS)),
+            dma((4,)),
             *deep_bufs,
             *deep_sems,
             *wide_bufs,
@@ -920,10 +1117,10 @@
             *gain_sems,
         ],
         compiler_params=pltpu.CompilerParams(
-            collective_id=2, has_side_effects=True, vmem_limit_bytes=66_000_000
+            collective_id=2, has_side_effects=True, vmem_limit_bytes=67_043_328
         ),
-        name="reduce_gradients",
-    )(*lefts, *rights, gain_grads)
+        name="backward_reduce",
+    )(*lefts, *weights, pre, *heads, middle, *small)
 
 
 def body(
@@ -948,72 +1145,45 @@
     device = lax.axis_index(("shard", "replica"))
     segment, position = locate(device, seq_lengths, seq_device, seq_offsets, rows)
     live = (segment >= 0).astype(jnp.float32)[:, None]
-    field = tokens.astype(jnp.float32)
     cosine, sine = rope_tables(position)
     allowed = mask_of(segment)
 
+    cosine, sine = jnp.tile(cosine, (1, 4)), jnp.tile(sine, (1, 4))
+    allowed = allowed.astype(jnp.float32)
     (
         w_qkv,
         w_out,
         w_gate_up,
         w_down,
-        normed_a_t,
-        mixed_t,
-        normed_m_t,
-        hidden_t,
-        roped,
-        total,
+        normed_a,
+        mixed,
+        normed_m,
+        hidden,
+        lse,
         middle,
         pre,
         gains,
+        *heads,
     ) = gather_forward(
         n_shard,
         (w_qkv, w_out, w_gate_up, w_down),
         jnp.concatenate([norm_attn, norm_mlp], axis=0).astype(jnp.float32),
         tokens,
-        jnp.tile(cosine, (1, 4)),
-        jnp.tile(sine, (1, 4)),
-        allowed.astype(jnp.float32),
+        cosine,
+        sine,
+        allowed,
     )
-    gains = gains.transpose(1, 0, 2).reshape(2, model)
-    gain_attn, gain_mlp = gains[0], gains[1]
-    per = HEADS // KV_HEADS
-    queries_b = roped[:, : HEADS * HEAD].reshape(rows, HEADS, HEAD)
-    keys_b = roped[:, HEADS * HEAD : (HEADS + KV_HEADS) * HEAD].reshape(rows, KV_HEADS, HEAD)
-    values_b = roped[:, (HEADS + KV_HEADS) * HEAD :].reshape(rows, KV_HEADS, HEAD)
-    total = total[:, :HEADS].T.reshape(KV_HEADS, per, rows, 1)
-    scale_a, scale_m = rms_scale(field), rms_scale(middle)
-    gate, upper = pre[:, :FF], pre[:, FF:]
-    result = ((middle + contract_rows(hidden_t, w_down)) * live).astype(jnp.bfloat16)
-
-    grad_field = cotangent.astype(jnp.float32) * live
-    grad_last = grad_field.astype(jnp.bfloat16)
-    grad_hidden = contract_cols(grad_last, w_down)
-    grad_pre = jnp.concatenate(gate_back(grad_hidden, gate, upper), axis=1)
-    grad_input, grad_gain_mlp = norm_back(
-        contract_cols(grad_pre, w_gate_up), middle, scale_m, gain_mlp
-    )
-    grad_middle = grad_field + grad_input
-
-    grad_branch = grad_middle.astype(jnp.bfloat16)
-    grad_mixed = contract_cols(grad_branch, w_out).astype(jnp.bfloat16)
-    grad_queries, grad_keys, grad_values = attend_backward(
-        grad_mixed, queries_b, keys_b, values_b, total, allowed
-    )
-    grad_project = join_grads(grad_queries, grad_keys, grad_values, cosine, sine)
-    grad_input, grad_gain_attn = norm_back(
-        contract_cols(grad_project, w_qkv), field, scale_a, gain_attn
-    )
-    grad_tokens = grad_middle + grad_input
-
-    gain_grads = jnp.stack([grad_gain_attn, grad_gain_mlp]).reshape(2, n_shard, owned_rows)
-    gain_grads = jnp.pad(gain_grads.transpose(1, 0, 2), ((0, 0), (0, 6), (0, 0)))
-    grad_down, grad_gate_up, grad_qkv, grad_out, gain_own = reduce_all(
+    result = ((middle + contract_rows(hidden, w_down)) * live).astype(jnp.bfloat16)
+    grad_last = (cotangent.astype(jnp.float32) * live).astype(jnp.bfloat16)
+    grad_down, grad_gate_up, grad_out, grad_qkv, gain_own, grad_tokens = backward_all(
         n_shard,
         n_replica,
-        [hidden_t, normed_m_t, normed_a_t, mixed_t],
-        [grad_last, grad_pre, grad_project, grad_branch],
-        gain_grads,
+        [hidden, normed_m, mixed, normed_a],
+        [w_down, w_gate_up, w_out, w_qkv],
+        pre,
+        heads,
+        middle,
+        [grad_last, tokens, gains, lse, cosine[:, :128], sine[:, :128], allowed],
     )
     grad_down, grad_gate_up, grad_qkv, grad_out = [
         grad.astype(jnp.float32) for grad in (grad_down, grad_gate_up, grad_qkv, grad_out)

time: 553 us -> 483 us (0.87); the launches traced: 543 us -> 483 us
  matrix products: 51.9 us -> 9.99 us
  Pallas kernels: 428 us -> 448 us
  local copies, waits for them, and re-layouts: 23.9 us -> 4.43 us
  other arithmetic: 38 us -> 19.6 us
    dot_general x9 -> x0, matrix products: 47.6 us -> none  [the longest x4 35.6 us: contract_cols(): lax.dot_general(left, right, (((1,), (1,)), ((), ())), preferred_element_...]
    pallas_call x1, Pallas kernels: 258 us -> 278 us  [backward_all(): pl.pallas_call(functools.partial(backward_kernel, n_shard, n_replica), ou...]
    concatenate x3 -> x1, other arithmetic: 6.63 us -> 0.02 us  [rope_tables(): jnp.concatenate([cosine, cosine], axis=-1)]
    dot_general x1, matrix products: 4.31 us -> 9.99 us  [contract_rows(): lax.dot_general(left, right, (((0,), (0,)), ((), ())), preferred_element_...]
where the time goes in v1:
time: 483 us
  Pallas kernels  448 us (93%)
  other arithmetic  19.6 us (4%)
  matrix products  9.99 us (2%)
    pallas_call x1, Pallas kernels, backward_all(): pl.pallas_call(functools.partial(backward_kernel, n_shard, n_replica), ou...  278 us
    pallas_call x1, Pallas kernels, gather_forward(): pl.pallas_call(functools.partial(forward_kernel, n_shard, plan, stages),...  170 us
    dot_general x1, matrix products, contract_rows(): lax.dot_general(left, right, (((0,), (0,)), ((), ())), preferred_element_...  9.99 us

profile of v1, /device:TPU:0, one launch (start us, length us, event | category | flops | bytes accessed | tf_op | source)
XLA Modules:
  0.0 483.1 jit_solution(13001252226501459519)
XLA Ops:
  0.6 0.0 copy-start.6
  0.6 0.7 broadcast_compare_fusion
  1.4 0.7 broadcast_multiply_fusion
  2.1 0.1 select_reduce_fusion
  2.2 0.0 copy-start.7
  2.2 1.3 maximum_convert_fusion.refs_4_
  3.5 0.3 multiply_sine_fusion
  3.8 0.8 fusion.3.refs_8_.refs_19_
  4.6 0.2 copy.23.refs_6_
  4.8 0.0 copy-start.2
  4.8 0.7 slice.16.refs_17_
  5.6 0.2 copy.24.refs_7_
  5.7 0.0 copy-start.3
  5.8 0.7 slice.17.refs_18_
  6.5 0.0 copy-done.7
  6.5 0.0 copy-done.6
  6.5 1.1 multiply_convert_fusion.refs_13_
  7.5 0.0 copy-done.2
  7.5 0.0 copy-done.3
  7.5 170.0 %gather_forward.1 = (bf16[1536,3072]{1,0:T(8,128)(2,1)}, bf16[1536,1536]{1,0:T(8,128)(2,1)}, bf16[1536,8192]{1,0:T(8,128)(2,1)}, bf16[4096,1536]{1,0:T(8,128)(2,...) custom-call(bf16[384,3072]{1,0:T(8,128)(2,1)} %bitcast.24, ...), custom_call_target="tpu_custom_call" | custom-call | tf_op jit(solution)/shard_map/gather_forward/pallas_call | solution.py:464
  177.5 278.4 %backward_reduce.1 = (bf16[1024,1536]{1,0:T(8,128)(2,1)}, bf16[384,8192]{1,0:T(8,128)(2,1)}, bf16[384,1536]{1,0:T(8,128)(2,1)}, bf16[384,3072]{1,0:T(8,128)(2,1)...) custom-call(bf16[4096,256]{1,0:T(8,128)(2,1)} %get-tuple-element.30.refs_0_, bf16[1536,256]{1,0:T(8,128)(2,1)} %get-tuple-element.32.refs_1_, ...), custom_call_target="tpu_custom_call" | custom-call | tf_op jit(solution)/shard_map/backward_reduce/pallas_call | solution.py:1073
  455.9 0.0 copy-start.5
  455.9 10.0 %fusion.1 = bf16[256,1536]{1,0:T(8,128)(2,1)} fusion(f32[256,1536]{1,0:T(8,128)} %get-tuple-element.29.refs_12_, bf16[4096,256]{1,0:T(8,128)(2,1)} %get-tuple-element.30.refs_0_, bf16[4096,1536]{1,0:T(8,128)(2,1)} %get-tuple-element.31.refs_4_, f32[256]{0:T(256)} %copy-done.7), kind=kOutput, calls=%fused_computation.4 | convolution fusion | flops 3222405120 | bytes 17040384 | tf_op jit(solution)/shard_map/dot_general | solution.py:49
  465.9 1.4 fusion.7
  467.4 0.0 copy-done.5
  467.4 1.7 bitcast_convert_fusion.3
  469.1 0.0 copy-done.1
  469.1 3.0 bitcast_convert_fusion.2
  472.0 3.6 bitcast_convert_fusion.1
  475.6 6.3 %bitcast_convert_fusion = f32[1,384,8192]{2,1,0:T(8,128)} fusion(bf16[384,8192]{1,0:T(8,128)(2,1)S(1)} %bitcast.22), kind=kLoop, calls=%fused_computation | loop fusion | flops 3145728 | bytes 18874368 | tf_op jit(solution)/shard_map/broadcast_in_dim | solution.py:1198
  482.0 0.0 copy-done.4
  482.0 1.1 copy.28
  (15 shorter events, 0.1 us)
Async XLA Ops:
  0.6 5.8 %copy-start.6 = (bf16[256,1536]{1,0:T(8,128)(2,1)S(1)}, bf16[256,1536]{1,0:T(8,128)(2,1)}, u32[]{:S(2)}) copy-start(bf16[256,1536]{1,0:T(8,128)(2,1)} %param.12) | copy-start | bytes 2359300
  2.2 4.2 copy-start.7
  4.8 2.7 copy-start.2
  5.7 1.8 copy-start.3
  455.9 11.4 %copy-start.5 = (bf16[384,1536]{1,0:T(8,128)(2,1)S(1)}, bf16[384,1536]{1,0:T(8,128)(2,1)}, u32[]{:S(2)}) copy-start(bf16[384,1536]{1,0:T(8,128)(2,1)} %get-tuple-element.47) | copy-start | bytes 3538948
  465.9 3.1 copy-start.1
  467.4 4.7 copy-start
  469.1 6.6 %slice-start = ((s8[6291456]{0:T(1024)(128)(4,1)}), s8[4194304]{0:T(1024)(128)(4,1)S(1)}, s32[]{:S(2)}) async-start(s8[6291456]{0:T(1024)(128)(4,1)} %bitcast.21), calls=%async_computation | async-start | bytes 8388608
  472.0 3.6 slice-start.1
  475.6 6.3 %copy-start.4 = (f32[256,1536]{1,0:T(8,128)S(1)}, f32[256,1536]{1,0:T(8,128)}, u32[]{:S(2)}) copy-start(f32[256,1536]{1,0:T(8,128)} %get-tuple-element.69) | copy-start | bytes 4718596

commit v2 on v1

--- a/solution.py
+++ b/solution.py
@@ -43,12 +43,6 @@
 def mask_of(segment):
     local = jnp.arange(segment.shape[0], dtype=jnp.int32)
     return (segment[:, None] == segment[None, :]) & (local[None, :] <= local[:, None])
-
-
-def contract_rows(left, right):
-    return lax.dot_general(
-        left, right, (((0,), (0,)), ((), ())), preferred_element_type=jnp.float32
-    )
 
 
 def gate_back(grad_hidden, gate, upper):
@@ -518,7 +512,9 @@
 
 
 class Pipe:
-    def __init__(self, n_shard, n_replica, begin, count, block, deliver, bufs, sems):
+    def __init__(self, n_shard, n_replica, begin, count, block, deliver, bufs, sems, pause=(0, 0)):
+        self.pause = pause
+        count = count + pause[1]
         self.shard, self.replica = lax.axis_index("shard"), lax.axis_index("replica")
         chip = self.replica // 2
         self.inner = lax.rem(chip, 2) != lax.rem(chip // 2, 2)
@@ -677,9 +673,17 @@
         for number in range(self.last + 2):
             chunk = time - self.begin - number
 
-            @pl.when((chunk >= 0) & (chunk < self.count))
+            @pl.when((chunk >= 0) & (chunk < self.count) & self.busy(chunk))
             def _(number=number, chunk=chunk):
                 self.stage(number, chunk, lax.rem(chunk, SLOTS))
+
+    def busy(self, chunk):
+        first, skip = self.pause
+        return (chunk < first) | (chunk >= first + skip)
+
+    def number(self, chunk):
+        first, skip = self.pause
+        return chunk - jnp.where(chunk < first, 0, skip)
 
     def length(self):
         return self.begin + self.count + self.last + 1
@@ -707,8 +711,8 @@
     take = lambda n: [refs.pop(0) for _ in range(n)]
     lefts, (w_down, w_gate_up, w_out, w_qkv, pre) = take(4), take(5)
     heads_in, middle_in = take(3), take(1)[0]
-    grad_last, tokens, gain, lse, cosine, sine, mask = take(7)
-    outs, (gain_out, grad_tokens) = take(4), take(2)
+    grad_last, tokens, gain, lse, cosine, sine, mask, live = take(8)
+    outs, (gain_out, grad_tokens, result) = take(4), take(3)
     deep_left, deep_right, wide_left, wide_right, other_right = take(5)
     tile_down, tile_up, tile_pre, tile_out = take(4)
     q_heads, k_heads, v_heads, middle, grad_middle, total, branch, joined, parts, gain_in = take(10)
@@ -779,6 +783,7 @@
         copy.start()
     deep_right[pl.ds(0, rows), :] = grad_last[:, half_of(0, core)]
     total[...] = jnp.zeros_like(total)
+    grad_middle[...] = jnp.zeros_like(grad_middle)
     gain_in[...] = jnp.zeros_like(gain_in)
     tile_out[...] = jnp.zeros_like(tile_out)
 
@@ -828,6 +833,9 @@
         total[...] += times_cols(grad_gate, tile_up[slot, 0]) + times_cols(
             grad_upper, tile_up[slot, 1]
         )
+        grad_middle[...] += times_rows(deep_left[span, pl.ds(0, rows)], tile_down[slot])
+
+    showing = pltpu.make_async_copy(joined.at[:, pl.ds(0, model)], result, late_sem.at[4])
 
     def norm_gradient(field, row):
         scale = lax.rsqrt(jnp.mean(field * field, axis=-1, keepdims=True) + epsilon)
@@ -854,6 +862,8 @@
             copy.wait()
         for n in range(EARLY - 4, EARLY):
             tile_pass(n).wait_send()
+        joined[:, :model] = ((middle[...] + grad_middle[...]) * live[...]).astype(jnp.bfloat16)
+        showing.start()
         grad_middle[...] = grad_last[...].astype(jnp.float32) + norm_gradient(middle[...], 1)
         branch[...] = grad_middle[...].astype(jnp.bfloat16)
         share_right(2, branch, 5).start()
@@ -919,6 +929,7 @@
     quad = 4 * HEAD
 
     def join():
+        showing.wait()
         for group in range(wide // quad):
             value = jnp.zeros((rows, quad), jnp.float32)
             for n in range(4):
@@ -958,6 +969,7 @@
         grad_tokens[...] = grad_middle[...] + norm_gradient(tokens[...].astype(jnp.float32), 0)
 
     def deep_block(chunk, other):
+        chunk = deep.number(chunk)
         start = (shard ^ other) * (2 * deep_rows) + (chunk // (n_deep // 2)) * deep_rows
         left = deep_left[pl.ds(pl.multiple_of(start, 16), deep_rows), :]
         cols = lax.rem(chunk, n_deep // 2) * DEEP_COLS
@@ -981,6 +993,7 @@
             copy.wait()
 
     def deep_deliver(chunk, side, src, sem, begin):
+        chunk = deep.number(chunk)
         half = core if side == 0 else 1 - core
         first = pl.multiple_of((chunk // (n_deep // 2)) * deep_rows, 16)
         start = half * halves[0] + lax.rem(chunk, n_deep // 2) * DEEP_COLS
@@ -1002,9 +1015,12 @@
     join_at = between_at + 1 + KV_HEADS
     end_at = join_at + 1 + n_last
     size = (n_shard, n_replica)
-    deep = Pipe(*size, 0, n_deep, deep_block, deep_deliver, deep_bufs, deep_sems)
+    wide_at = 2 * n_deep // 3
+    deep = Pipe(
+        *size, 0, n_deep, deep_block, deep_deliver, deep_bufs, deep_sems, (wide_at, edges[3])
+    )
     wide_pipe = Pipe(
-        *size, n_deep, edges[3], wide_block, wide_deliver, wide_bufs, wide_sems
+        *size, wide_at, edges[3], wide_block, wide_deliver, wide_bufs, wide_sems
     )
     gain_pipe = Pipe(
         *size, end_at + 1, 1, lambda chunk, other: gain_in[shard ^ other], gain_deliver, gain_bufs, gain_sems
@@ -1023,15 +1039,15 @@
             def _():
                 run(time - first)
 
-        @pl.when(time == n_deep)
+        @pl.when(time == wide_at)
         def _():
             for k in range(1, 4):
                 loads[k].wait()
                 passes[k + 1].wait()
 
-        at(n_deep, EARLY, lambda n: tile_pass(n).wait_recv())
-        at(n_deep + edges[1], 1, lambda n: share_wait(2, branch, 5))
-        at(n_deep + edges[2], 1, lambda n: share_wait(3, joined, 6))
+        at(wide_at, EARLY, lambda n: tile_pass(n).wait_recv())
+        at(wide_at + edges[1], 1, lambda n: share_wait(2, branch, 5))
+        at(wide_at + edges[2], 1, lambda n: share_wait(3, joined, 6))
         deep.run(time)
         wide_pipe.run(time)
         gain_pipe.run(time)
@@ -1052,7 +1068,7 @@
             index,
         ).wait()
 
-    lax.fori_loop(0, max(wide_pipe.length(), gain_pipe.length()), step, 0)
+    lax.fori_loop(0, max(deep.length(), wide_pipe.length(), gain_pipe.length()), step, 0)
 
 
 def backward_all(n_shard, n_replica, lefts, weights, pre, heads, middle, small):
@@ -1078,9 +1094,10 @@
         + [
             jax.ShapeDtypeStruct((8, owned[1]), f32),
             jax.ShapeDtypeStruct((rows, model), f32),
+            jax.ShapeDtypeStruct((rows, model), bf16),
         ],
-        in_specs=[anywhere] * 13 + [whole] * 7,
-        out_specs=[anywhere] * 4 + [whole] * 2,
+        in_specs=[anywhere] * 13 + [whole] * 8,
+        out_specs=[anywhere] * 4 + [whole] * 2 + [anywhere],
         scratch_shapes=[
             pltpu.VMEM((hidden, 2 * rows), bf16),
             pltpu.VMEM((2 * rows, model // 2), bf16),
@@ -1108,7 +1125,7 @@
             dma((EARLY,)),
             dma((2, 5)),
             dma((2, HEADS // KV_HEADS)),
-            dma((4,)),
+            dma((5,)),
             *deep_bufs,
             *deep_sems,
             *wide_bufs,
@@ -1173,9 +1190,8 @@
         sine,
         allowed,
     )
-    result = ((middle + contract_rows(hidden, w_down)) * live).astype(jnp.bfloat16)
     grad_last = (cotangent.astype(jnp.float32) * live).astype(jnp.bfloat16)
-    grad_down, grad_gate_up, grad_out, grad_qkv, gain_own, grad_tokens = backward_all(
+    grad_down, grad_gate_up, grad_out, grad_qkv, gain_own, grad_tokens, result = backward_all(
         n_shard,
         n_replica,
         [hidden, normed_m, mixed, normed_a],
@@ -1183,7 +1199,7 @@
         pre,
         heads,
         middle,
-        [grad_last, tokens, gains, lse, cosine[:, :128], sine[:, :128], allowed],
+        [grad_last, tokens, gains, lse, cosine[:, :128], sine[:, :128], allowed, live],
     )
     grad_down, grad_gate_up, grad_qkv, grad_out = [
         grad.astype(jnp.float32) for grad in (grad_down, grad_gate_up, grad_qkv, grad_out)

time: 483 us -> 476 us (0.986)
  matrix products: 9.99 us -> 0 us
    dot_general x1 -> x0, matrix products: 9.99 us -> none  [contract_rows(): lax.dot_general(left, right, (((0,), (0,)), ((), ())), preferred_element_...]
where the time goes in v2:
time: 476 us; the launch traced here: 475 us
  Pallas kernels  447 us (94%)
  other arithmetic  21 us (4%)
  local copies, waits for them, and re-layouts  6.11 us (1%)
    pallas_call x1, Pallas kernels, backward_all(): pl.pallas_call(functools.partial(backward_kernel, n_shard, n_replica), ou...  277 us
    pallas_call x1, Pallas kernels, gather_forward(): pl.pallas_call(functools.partial(forward_kernel, n_shard, plan, stages),...  170 us

profile of v2, /device:TPU:0, one launch (start us, length us, event | category | flops | bytes accessed | tf_op | source)
XLA Modules:
  0.0 475.3 jit_solution(12769982948043366150)
XLA Ops:
  0.6 0.0 copy-start.6
  0.6 0.7 broadcast_compare_fusion
  1.4 0.7 broadcast_multiply_fusion
  2.1 0.1 select_reduce_fusion
  2.2 1.3 maximum_convert_fusion.refs_4_
  3.5 0.3 multiply_sine_fusion
  3.8 0.8 copy.28.refs_20_
  4.6 0.8 fusion.1.refs_8_.refs_19_
  5.4 0.2 copy.24.refs_6_
  5.6 0.0 copy-start.2
  5.6 0.7 slice.16.refs_17_
  6.3 0.2 copy.25.refs_7_
  6.5 0.0 copy-start.3
  6.5 0.7 slice.17.refs_18_
  7.2 0.0 copy-done.6
  7.2 1.1 multiply_convert_fusion.refs_13_
  8.3 0.0 copy-done.2
  8.3 0.0 copy-done.3
  8.3 170.0 %gather_forward.1 = (bf16[1536,3072]{1,0:T(8,128)(2,1)}, bf16[1536,1536]{1,0:T(8,128)(2,1)}, bf16[1536,8192]{1,0:T(8,128)(2,1)}, bf16[4096,1536]{1,0:T(8,128)(2,...) custom-call(bf16[384,3072]{1,0:T(8,128)(2,1)} %bitcast.23, ...), custom_call_target="tpu_custom_call" | custom-call | tf_op jit(solution)/shard_map/gather_forward/pallas_call | solution.py:458
  178.3 277.5 %backward_reduce.1 = (bf16[1024,1536]{1,0:T(8,128)(2,1)}, bf16[384,8192]{1,0:T(8,128)(2,1)}, bf16[384,1536]{1,0:T(8,128)(2,1)}, bf16[384,3072]{1,0:T(8,128)(2,1)...) custom-call(bf16[4096,256]{1,0:T(8,128)(2,1)} %get-tuple-element.30.refs_0_, ...), custom_call_target="tpu_custom_call" | custom-call | tf_op jit(solution)/shard_map/backward_reduce/pallas_call | solution.py:1089
  455.8 0.0 copy-start.1
  455.8 1.4 fusion.5
  457.3 3.1 bitcast_convert_fusion.3
  460.4 0.0 copy-done.1
  460.4 3.0 bitcast_convert_fusion.2
  463.4 0.0 copy-done
  463.4 3.6 bitcast_convert_fusion.1
  466.9 0.0 slice-done
  466.9 0.0 slice-done.1
  467.0 6.3 %bitcast_convert_fusion = f32[1,384,8192]{2,1,0:T(8,128)} fusion(bf16[384,8192]{1,0:T(8,128)(2,1)S(1)} %bitcast.21), kind=kLoop, calls=%fused_computation | loop fusion | flops 3145728 | bytes 18874368 | tf_op jit(solution)/shard_map/broadcast_in_dim | solution.py:1214
  473.3 0.9 copy.31
  474.2 1.1 copy.32
  (14 shorter events, 0.1 us)
Async XLA Ops:
  0.6 6.6 %copy-start.6 = (bf16[256,1536]{1,0:T(8,128)(2,1)S(1)}, bf16[256,1536]{1,0:T(8,128)(2,1)}, u32[]{:S(2)}) copy-start(bf16[256,1536]{1,0:T(8,128)(2,1)} %param.12) | copy-start | bytes 2359300
  5.6 2.7 copy-start.2
  6.5 1.8 copy-start.3
  455.8 4.6 copy-start.1
  457.3 6.1 %copy-start = (bf16[1024,1536]{1,0:T(8,128)(2,1)S(1)}, bf16[1024,1536]{1,0:T(8,128)(2,1)}, u32[]{:S(2)}) copy-start(bf16[1024,1536]{1,0:T(8,128)(2,1)} %get-tuple-element.51) | copy-start | bytes 9437188
  460.4 6.5 %slice-start = ((s8[6291456]{0:T(1024)(128)(4,1)}), s8[4194304]{0:T(1024)(128)(4,1)S(1)}, s32[]{:S(2)}) async-start(s8[6291456]{0:T(1024)(128)(4,1)} %bitcast.20), calls=%async_computation | async-start | bytes 8388608
  463.4 3.6 slice-start.1
  466.9 6.3 %copy-start.5 = (bf16[256,1536]{1,0:T(8,128)(2,1)S(1)}, bf16[256,1536]{1,0:T(8,128)(2,1)}, u32[]{:S(2)}) copy-start(bf16[256,1536]{1,0:T(8,128)(2,1)} %get-tuple-element.70) | copy-start | bytes 2359300
  467.0 7.2 %copy-start.4 = (f32[256,1536]{1,0:T(8,128)S(1)}, f32[256,1536]{1,0:T(8,128)}, u32[]{:S(2)}) copy-start(f32[256,1536]{1,0:T(8,128)} %get-tuple-element.71) | copy-start | bytes 4718596
